TPU v7x, 32 devices: a whole 2x2x4 slice. The times are simulated.
32 devices in a mesh: band: 4 (over y, core), grid: 8 (over z, x).
Axes of the slice: x: 2, y: 2, z: 4, core: 2. Of those that a mesh axis runs over, the one named last changes fastest.
Arguments:
- orbitals: bfloat16 [64, 2, 16, 128, 128], P('band', None, 'grid'), may hold values from -1.5 to 1.5
- occupations: float32 [64], P('band'), may hold values from 0.2 to 2
Outputs:
- current: float32 [3, 16, 128, 128], P(None, 'grid', 'band')
All inputs are finite; a program needn't handle non-finite values.
Results may differ from a plain program's by a relative error of at most 0.0003.
Values may be sent and summed in bfloat16 or wider, within the bound.
No kernel may reach another device: no remote copies, remote signals or barrier semaphores. Data moves between devices by JAX's collectives and lax.ppermute only.
A program may use at most 64 MiB of HBM per device.

v0:
```python
import functools

import jax
import jax.numpy as jnp
import numpy as np
from jax import lax
from jax.experimental import pallas as pl
from jax.experimental.pallas import tpu as pltpu
from jax.sharding import PartitionSpec as P


ODD, CORNER, CORE, HALF = range(4, 8)


def stencil(cells):
    eye = np.eye(cells, dtype=np.float32)
    near = np.roll(eye, 1, 0) - np.roll(eye, -1, 0)
    far = np.roll(eye, 2, 0) - np.roll(eye, -2, 0)
    return jnp.asarray(8.0 * near - far, jnp.bfloat16)


def lateral_kernel(weights, *rest):
    quarters, (across, along, kept, sent, spread, field, total) = rest[:4], rest[4:]
    bands, parts, planes, rows, _ = quarters[0].shape
    table = places()
    total[...] = jnp.zeros_like(total)
    dot = functools.partial(jnp.dot, preferred_element_type=jnp.float32)

    def advance(n, carry):
        weight = weights[n]
        for i, quarter in enumerate(quarters):
            at = pl.ds(pl.multiple_of(table[i] * rows, rows), rows)
            for part in range(parts):
                for plane in range(planes):
                    field[part, plane, at] = quarter[n, part, plane]
        fields = []
        for plane in range(planes):
            re16 = field[0, plane]
            im16 = field[1, plane]
            re = weight * re16.astype(jnp.float32)
            im = weight * im16.astype(jnp.float32)
            fields.append((re, im, re16, im16))
            total[1 + plane] += re * dot(across[...], im16) - im * dot(across[...], re16)
            total[3 + plane] += re * dot(im16, along[...]) - im * dot(re16, along[...])
        (re, im, _, _), (_, _, re_up, im_up) = fields
        total[0] += 8.0 * (re * im_up.astype(jnp.float32) - im * re_up.astype(jnp.float32))
        return carry

    lax.fori_loop(0, bands, advance, 0)
    for n in range(bands):
        spread[n : n + 1] = jnp.full((1, spread.shape[1]), weights[n], jnp.float32)
    core = table[CORE]
    for half in range(2):
        for out, row in ((kept, 2 * half + core), (sent, 2 * half + 1 - core)):
            at = pl.ds(pl.multiple_of(row * rows, rows), rows)
            out[half] = total[:, at] * (1.0 / 12.0)


def lateral(quarters, weights):
    bands, parts, planes, rows, ny = quarters[0].shape
    nx = 4 * rows
    smem = pl.BlockSpec(memory_space=pltpu.SMEM)
    vmem = pl.BlockSpec(memory_space=pltpu.VMEM)
    return pl.pallas_call(
        lateral_kernel,
        in_specs=[smem] + [vmem] * 6,
        out_specs=[vmem] * 3,
        out_shape=[jax.ShapeDtypeStruct((2, 5, rows, ny), jnp.float32)] * 2
        + [jax.ShapeDtypeStruct((bands, ny), jnp.float32)],
        scratch_shapes=[
            pltpu.VMEM((parts, planes, nx, ny), quarters[0].dtype),
            pltpu.VMEM((5, nx, ny), jnp.float32),
        ],
        compiler_params=pltpu.CompilerParams(vmem_limit_bytes=8 << 20),
        name="lateral",
    )(weights, *quarters, stencil(nx).T, stencil(ny))


def places():
    odd = lax.axis_index("grid") % 2
    group = lax.axis_index("band")
    core = group % 2
    half = group // 2
    quarters = (
        2 * (1 - odd) + core,
        2 * odd + core,
        2 * (1 - odd) + 1 - core,
        2 * odd + 1 - core,
    )
    corner = jnp.where(half == odd, 0, 1)
    return quarters + (odd, corner, core, half)


def split_kernel(first, orbitals, *rest):
    outs, flags, sem = rest[:2], rest[2], rest[3]
    rows = outs[0].shape[3]
    table = places()
    copies = [
        pltpu.make_async_copy(
            orbitals.at[:, :, :, pl.ds(pl.multiple_of(table[first + i] * rows, rows), rows)], out, sem.at[i]
        )
        for i, out in enumerate(outs)
    ]
    for copy in copies:
        copy.start()
    for i, place in enumerate(table):
        flags[i : i + 1] = jnp.full((1, flags.shape[1]), place, jnp.int32)
    for copy in copies:
        copy.wait()


def split(first, orbitals):
    bands, parts, planes, nx, ny = orbitals.shape
    return pl.pallas_call(
        functools.partial(split_kernel, first),
        in_specs=[pl.BlockSpec(memory_space=pltpu.HBM)],
        out_specs=[pl.BlockSpec(memory_space=pltpu.VMEM)] * 3,
        out_shape=[pltpu.VMEM((bands, parts, planes, nx // 4, ny), orbitals.dtype)] * 2
        + [pltpu.VMEM((8, ny), jnp.int32)],
        scratch_shapes=[pltpu.SemaphoreType.DMA((2,))],
        compiler_params=pltpu.CompilerParams(vmem_limit_bytes=4 << 20),
        name="split",
    )(pltpu.with_memory_space_constraint(orbitals, pltpu.HBM))


def halve_kernel(flags, mine, theirs, kept, sent):
    lower = jnp.broadcast_to(flags[HALF : HALF + 1], kept.shape[1:]) == 0
    for i in range(kept.shape[0]):
        low = mine[0, i] + theirs[0, i]
        high = mine[1, i] + theirs[1, i]
        kept[i] = jnp.where(lower, low, high)
        sent[i] = jnp.where(lower, high, low)


def edges(odd, weights, first, second, sums):
    def advance(n, sums):
        def field(rows, scale=None):
            values = [[rows[n, part, k].astype(jnp.float32) for part in range(2)] for k in range(2)]
            if scale is not None:
                values = [[scale * value for value in plane] for plane in values]
            return values

        def pick(low, high):
            return [jnp.where(odd, a, b) for a, b in zip(low, high)]

        def term(low, high):
            return low[0] * high[1] - low[1] * high[0]

        f, g = field(first, weights[pl.ds(n, 1)]), field(second)
        new = (
            term(f[0], g[0]),
            term(f[1], g[1]),
            term(pick(f[0], f[1]), pick(g[1], g[0])),
        )
        return tuple(a + b for a, b in zip(sums, new))

    sums = tuple(sums[i] for i in range(3))
    return lax.fori_loop(0, first.shape[0], advance, sums, unroll=UNROLL)


def flag(flags, which, shape):
    return jnp.broadcast_to(flags[which : which + 1], shape) == 1


def scaled(odd, sums):
    sign = jnp.where(odd, -1.0 / 12.0, 1.0 / 12.0)
    low, high, mid = sums
    up = jnp.where(odd, -8.0 / 12.0, 0.0) * mid
    down = jnp.where(odd, 0.0, 8.0 / 12.0) * mid
    return (up - sign * low, down - sign * high), (down - sign * low, up - sign * high)


def first_kernel(flags, weights, own, side, far, inner, outer):
    shape = inner.shape[1:]
    odd = flag(flags, ODD, shape)
    zero = (jnp.zeros(shape, jnp.float32),) * 3
    for out, pair in ((inner, (own, side)), (outer, (side, far))):
        for i, value in enumerate(edges(odd, weights, *pair, zero)):
            out[i] = value


def inner_kernel(flags, weights, own, side, sums, kept, near, inner_side):
    shape = kept.shape[1:]
    odd = flag(flags, ODD, shape)
    here = flag(flags, CORNER, shape)
    own_parts, side_parts = scaled(odd, edges(odd, weights, own, side, sums))
    for plane in range(2):
        kept[plane] = jnp.where(here, own_parts[plane], 0.0)
        near[plane] = jnp.where(here, side_parts[plane], own_parts[plane])
        inner_side[plane] = side_parts[plane]


def outer_kernel(flags, weights, side, far, sums, inner_side, middle, distant):
    shape = middle.shape[1:]
    odd = flag(flags, ODD, shape)
    here = flag(flags, CORNER, shape)
    side_parts, far_parts = scaled(odd, edges(odd, weights, side, far, sums))
    for plane in range(2):
        middle[plane] = jnp.where(here, far_parts[plane], side_parts[plane] + inner_side[plane])
        distant[plane] = jnp.where(here, side_parts[plane], far_parts[plane])


def call(kernel, arrays, out_shapes):
    vmem = pl.BlockSpec(memory_space=pltpu.VMEM)
    return pl.pallas_call(
        kernel,
        in_specs=[vmem] * len(arrays),
        out_specs=[vmem] * len(out_shapes),
        out_shape=[jax.ShapeDtypeStruct(shape, jnp.float32) for shape in out_shapes],
        compiler_params=pltpu.CompilerParams(vmem_limit_bytes=4 << 20),
    )(*arrays)


def finish_kernel(flat, flat_rest, kept, near, middle, distant, out):
    for plane in range(2):
        parts = kept[plane] + near[plane] + middle[plane] + distant[plane]
        out[0, plane] = flat[0] + flat_rest[0] + parts
        out[1, plane] = flat[1 + plane] + flat_rest[1 + plane]
        out[2, plane] = flat[3 + plane] + flat_rest[3 + plane]


def per_device(orbitals, occupations):
    slabs = lax.axis_size("grid")
    groups = lax.axis_size("band")
    assert groups == 4 and slabs % 2 == 0 and orbitals.shape[2] == 2

    def beyond(g):
        return (g + 2) % slabs if g % 2 else (g - 2) % slabs

    def home(g):
        return (g - 2) % slabs if g % 2 else (g + 2) % slabs

    def route(value, target):
        pairs = []
        for b in range(groups):
            for g in range(slabs):
                goal = target(b, g)
                pairs.append((b * slabs + g, goal[0] * slabs + goal[1]))
        return lax.ppermute(value, ("band", "grid"), pairs)

    own, side, flags = split(0, orbitals)
    own_across, side_across, _ = split(2, orbitals)

    side1 = route(side, lambda b, g: (b, g ^ 1))
    far1 = route(own, lambda b, g: (b, beyond(g)))
    side2 = route(side_across, lambda b, g: (b ^ 1, g ^ 1))
    far2 = route(own_across, lambda b, g: (b ^ 1, beyond(g)))
    own2 = route(own_across, lambda b, g: (b ^ 1, g))

    plane = own.shape[-2:]
    mine, sent, spread = lateral((own, side, own_across, side_across), occupations)
    w2 = route(spread, lambda b, g: (b ^ 1, g))
    theirs = route(sent, lambda b, g: (b ^ 1, g))
    flat, sent = call(halve_kernel, (flags, mine, theirs), [(5,) + plane] * 2)
    flat_rest = route(sent, lambda b, g: (b ^ 2, g))

    inner, outer = call(
        first_kernel, (flags, spread, own, side1, far1), [(3,) + plane] * 2
    )
    kept, near, inner_side = call(inner_kernel, (flags, w2, own2, side2, inner), [(2,) + plane] * 3)

    def is_corner(b, g):
        return b // 2 != g % 2

    got_near = route(near, lambda b, g: (b, g ^ 1) if is_corner(b, g) else (b ^ 2, g))
    middle, distant = call(
        outer_kernel, (flags, w2, side2, far2, outer, inner_side), [(2,) + plane] * 2
    )
    got_middle = route(middle, lambda b, g: (b, home(g)) if is_corner(b, g) else (b ^ 2, g ^ 1))
    got_distant = route(distant, lambda b, g: (b, g ^ 1) if is_corner(b, g) else (b ^ 2, home(g)))
    arrays = (flat, flat_rest, kept, got_near, got_middle, got_distant)
    (out,) = call(finish_kernel, arrays, [(3, 2) + plane])
    return out


UNROLL = 4


def solution(mesh):
    placed = (P("band", None, "grid", None, None), P("band"))
    return jax.shard_map(
        per_device,
        mesh=mesh,
        in_specs=placed,
        out_specs=P(None, "grid", "band", None),
        check_vma=False,
    )
```

profile of v0, /device:TPU:0, one launch (start us, length us, event | category | flops | bytes accessed | tf_op | source)
XLA Modules:
  0.0 43.4 jit_solution(8088925982373998019)
XLA Ops:
  0.0 0.0 copy-start
  0.0 0.0 copy-start.1
  0.0 0.0 copy-start.2
  0.0 1.2 %split.2 = (bf16[16,2,2,32,128]{4,3,2,1,0:T(8,128)(2,1)S(1)}, bf16[16,2,2,32,128]{4,3,2,1,0:T(8,128)(2,1)S(1)}, s32[8,128]{1,0:T(8,128)S(1)}) custom-call(bf16[16,2,2,128,128]{4,3,2,1,0:T(8,128)(2,1)} %orbitals.3), custom_call_target="tpu_custom_call" | custom-call | tf_op jit(solution)/shard_map/split/pallas_call | solution.py:114
  1.2 1.8 %split.3 = (bf16[16,2,2,32,128]{4,3,2,1,0:T(8,128)(2,1)S(1)}, bf16[16,2,2,32,128]{4,3,2,1,0:T(8,128)(2,1)S(1)}, s32[8,128]{1,0:T(8,128)}) custom-call(bf16[16,2,2,128,128]{4,3,2,1,0:T(8,128)(2,1)} %orbitals.3), custom_call_target="tpu_custom_call" | custom-call | tf_op jit(solution)/shard_map/split/pallas_call | solution.py:114
  3.1 0.0 copy-done
  3.1 0.0 copy-done.1
  3.1 0.0 copy-done.2
  3.1 4.4 %lateral.1 = (f32[2,5,32,128]{3,2,1,0:T(8,128)S(1)}, f32[2,5,32,128]{3,2,1,0:T(8,128)S(1)}, f32[16,128]{1,0:T(8,128)S(1)}) custom-call(f32[16]{0:T(128)S(1)} %copy-done.2, bf16[16,2,2,32,128]{4,3,2,1,0:T(8,128)(2,1)S(1)} %get-tuple-element.23.rest_0_.own, bf16[16,2,2,32,128]{4,3,2,1,0:T(8,128)(2,1)S(1)} %get-tuple-element.24.rest_1_, ...), custom_call_target="tpu_custom_call" | custom-call | tf_op jit(solution)/shard_map/lateral/pallas_call | solution.py:64
  7.5 0.6 %collective-permute-start = (f32[2,5,32,128]{3,2,1,0:T(8,128)S(1)}, f32[2,5,32,128]{3,2,1,0:T(8,128)S(1)}, u32[]{:S(2)}, u32[]{:S(2)}) collective-permute-start(f32[2,5,32,128]{3,2,1,0:T(8,128)S(1)} %get-tuple-element.28), channel_id=1, source_target_pairs={{0,8},{1,9},{2,10},{3,11},{4,12},{5,13},{6,14},{7,15},{8,0},{9,1},... | collective-permute-start | bytes 491528 | tf_op jit(solution)/shard_map/ppermute | solution.py:239
  8.1 2.5 %collective-permute-start.5 = (bf16[16,2,2,32,128]{4,3,2,1,0:T(8,128)(2,1)S(1)}, bf16[16,2,2,32,128]{4,3,2,1,0:T(8,128)(2,1)S(1)}, u32[]{:S(2)}, u32[]{:S(2)}) collective-permute-start(bf16[16,2,2,32,128]{4,3,2,1,0:T(8,128)(2,1)S(1)} %get-tuple-element.24.rest_1_), channel_id=1, source_target_pairs={{0,1},{1,0},{2,3},{3,2},{4,5},{5,4},{6,7},{7,6},{8,9},{9,8},{10,11... | collective-permute-start | bytes 1572872 | tf_op jit(solution)/shard_map/ppermute | solution.py:239
  10.6 3.6 %collective-permute-start.6 = (bf16[16,2,2,32,128]{4,3,2,1,0:T(8,128)(2,1)S(1)}, bf16[16,2,2,32,128]{4,3,2,1,0:T(8,128)(2,1)S(1)}, u32[]{:S(2)}, u32[]{:S(2)}) collective-permute-start(bf16[16,2,2,32,128]{4,3,2,1,0:T(8,128)(2,1)S(1)} %get-tuple-element.23.rest_0_.own), channel_id=1, source_target_pairs={{0,6},{1,3},{2,0},{3,5},{4,2},{5,7},{6,4},{7,1},{8,14},{9,11},{10,... | collective-permute-start | bytes 1572872 | tf_op jit(solution)/shard_map/ppermute | solution.py:239
  14.2 0.0 collective-permute-start.3
  14.2 0.0 collective-permute-start.4
  14.2 0.0 collective-permute-done.theirs
  14.2 0.6 %collective-permute-start.8 = (bf16[16,2,2,32,128]{4,3,2,1,0:T(8,128)(2,1)S(1)}, bf16[16,2,2,32,128]{4,3,2,1,0:T(8,128)(2,1)S(1)}, u32[]{:S(2)}, u32[]{:S(2)}) collective-permute-start(bf16[16,2,2,32,128]{4,3,2,1,0:T(8,128)(2,1)S(1)} %get-tuple-element.25.rest_2_), channel_id=1, source_target_pairs={{0,14},{1,11},{2,8},{3,13},{4,10},{5,15},{6,12},{7,9},{8,6},{9,3},... | collective-permute-start | bytes 1572872 | tf_op jit(solution)/shard_map/ppermute | solution.py:239
  14.8 8.6 %collective-permute-done.5.side = bf16[16,2,2,32,128]{4,3,2,1,0:T(8,128)(2,1)S(1)} collective-permute-done((bf16[16,2,2,32,128]{4,3,2,1,0:T(8,128)(2,1)S(1)}, bf16[16,2,2,32,128]{4,3,2,1,0:T(8,128)(2,1)S(1)}, u32[]{:S(2)}, u32[]{:S(2)}) %collective-permute-start.5) | collective-permute-done | bytes 524320 | tf_op jit(solution)/shard_map/ppermute | solution.py:239
  23.4 2.1 %collective-permute-start.1 = (f32[5,32,128]{2,1,0:T(8,128)S(1)}, f32[5,32,128]{2,1,0:T(8,128)S(1)}, u32[]{:S(2)}, u32[]{:S(2)}) collective-permute-start(f32[5,32,128]{2,1,0:T(8,128)S(1)} %get-tuple-element.30), channel_id=1, source_target_pairs={{0,16},{1,17},{2,18},{3,19},{4,20},{5,21},{6,22},{7,23},{8,24},{9,... | collective-permute-start | bytes 245768 | tf_op jit(solution)/shard_map/ppermute | solution.py:239
  25.5 1.0 %collective-permute-done.6.far = bf16[16,2,2,32,128]{4,3,2,1,0:T(8,128)(2,1)S(1)} collective-permute-done((bf16[16,2,2,32,128]{4,3,2,1,0:T(8,128)(2,1)S(1)}, bf16[16,2,2,32,128]{4,3,2,1,0:T(8,128)(2,1)S(1)}, u32[]{:S(2)}, u32[]{:S(2)}) %collective-permute-start.6) | collective-permute-done | bytes 524320 | tf_op jit(solution)/shard_map/ppermute | solution.py:239
  26.5 0.0 collective-permute-start.2
  26.5 0.5 %shard_map.47 = (f32[3,32,128]{2,1,0:T(8,128)S(1)}, f32[3,32,128]{2,1,0:T(8,128)S(1)}) custom-call(s32[8,128]{1,0:T(8,128)S(1)} %get-tuple-element.22.flags, f32[16,128]{1,0:T(8,128)S(1)} %get-tuple-element.31.weights, bf16[16,2,2,32,128]{4,3,2,1,0:T(8,128)(2,1)S(1)} %get-tuple-element.23.rest_0_.own, ...), custom_call_target="tpu_custom_call" | custom-call | tf_op jit(solution)/shard_map/pallas_call | solution.py:205
  27.1 0.6 %collective-permute-done.2.weights = f32[16,128]{1,0:T(8,128)S(1)} collective-permute-done((f32[16,128]{1,0:T(8,128)S(1)}, f32[16,128]{1,0:T(8,128)S(1)}, u32[]{:S(2)}, u32[]{:S(2)}) %collective-permute-start.2) | collective-permute-done | bytes 8224 | tf_op jit(solution)/shard_map/ppermute | solution.py:239
  27.7 0.0 collective-permute-done.3.own
  27.7 6.4 %collective-permute-done.4.side = bf16[16,2,2,32,128]{4,3,2,1,0:T(8,128)(2,1)S(1)} collective-permute-done((bf16[16,2,2,32,128]{4,3,2,1,0:T(8,128)(2,1)S(1)}, bf16[16,2,2,32,128]{4,3,2,1,0:T(8,128)(2,1)S(1)}, u32[]{:S(2)}, u32[]{:S(2)}) %collective-permute-start.4) | collective-permute-done | bytes 524320 | tf_op jit(solution)/shard_map/ppermute | solution.py:239
  34.1 0.3 shard_map.48
  34.4 1.6 %collective-permute-start.7 = (f32[2,32,128]{2,1,0:T(8,128)S(1)}, f32[2,32,128]{2,1,0:T(8,128)S(1)}, u32[]{:S(2)}, u32[]{:S(2)}) collective-permute-start(f32[2,32,128]{2,1,0:T(8,128)S(1)} %get-tuple-element.34), channel_id=1, source_target_pairs={{0,16},{1,0},{2,18},{3,2},{4,20},{5,4},{6,22},{7,6},{8,24},{9,8},{... | collective-permute-start | bytes 98312 | tf_op jit(solution)/shard_map/ppermute | solution.py:239
  36.0 1.0 %collective-permute-done.8.far = bf16[16,2,2,32,128]{4,3,2,1,0:T(8,128)(2,1)S(1)} collective-permute-done((bf16[16,2,2,32,128]{4,3,2,1,0:T(8,128)(2,1)S(1)}, bf16[16,2,2,32,128]{4,3,2,1,0:T(8,128)(2,1)S(1)}, u32[]{:S(2)}, u32[]{:S(2)}) %collective-permute-start.8) | collective-permute-done | bytes 524320 | tf_op jit(solution)/shard_map/ppermute | solution.py:239
  37.0 0.3 shard_map.49
  37.2 1.6 %collective-permute-start.9 = (f32[2,32,128]{2,1,0:T(8,128)S(1)}, f32[2,32,128]{2,1,0:T(8,128)S(1)}, u32[]{:S(2)}, u32[]{:S(2)}) collective-permute-start(f32[2,32,128]{2,1,0:T(8,128)S(1)} %get-tuple-element.37), channel_id=1, source_target_pairs={{0,17},{1,7},{2,19},{3,1},{4,21},{5,3},{6,23},{7,5},{8,25},{9,15},... | collective-permute-start | bytes 98312 | tf_op jit(solution)/shard_map/ppermute | solution.py:239
  38.8 1.6 %collective-permute-start.10 = (f32[2,32,128]{2,1,0:T(8,128)S(1)}, f32[2,32,128]{2,1,0:T(8,128)S(1)}, u32[]{:S(2)}, u32[]{:S(2)}) collective-permute-start(f32[2,32,128]{2,1,0:T(8,128)S(1)} %get-tuple-element.38), channel_id=1, source_target_pairs={{0,18},{1,0},{2,20},{3,2},{4,22},{5,4},{6,16},{7,6},{8,26},{9,8},{... | collective-permute-start | bytes 98312 | tf_op jit(solution)/shard_map/ppermute | solution.py:239
  40.4 0.0 collective-permute-done.1.flat_rest
  40.4 0.0 collective-permute-done.7.near
  40.4 1.7 %collective-permute-done.9.middle = f32[2,32,128]{2,1,0:T(8,128)S(1)} collective-permute-done((f32[2,32,128]{2,1,0:T(8,128)S(1)}, f32[2,32,128]{2,1,0:T(8,128)S(1)}, u32[]{:S(2)}, u32[]{:S(2)}) %collective-permute-start.9) | collective-permute-done | bytes 32800 | tf_op jit(solution)/shard_map/ppermute | solution.py:239
  42.1 0.6 %collective-permute-done.10.distant = f32[2,32,128]{2,1,0:T(8,128)S(1)} collective-permute-done((f32[2,32,128]{2,1,0:T(8,128)S(1)}, f32[2,32,128]{2,1,0:T(8,128)S(1)}, u32[]{:S(2)}, u32[]{:S(2)}) %collective-permute-start.10) | collective-permute-done | bytes 32800 | tf_op jit(solution)/shard_map/ppermute | solution.py:239
  42.7 0.7 %shard_map.50 = f32[3,2,32,128]{3,2,1,0:T(8,128)} custom-call(f32[5,32,128]{2,1,0:T(8,128)S(1)} %get-tuple-element.29.flat, f32[5,32,128]{2,1,0:T(8,128)S(1)} %collective-permute-done.1.flat_rest, f32[2,32,128]{2,1,0:T(8,128)S(1)} %get-tuple-element.33.kept, f32[2,32,128]{2,1,0:T(8,128)S(1)} %collective-permute-done.7.near, ...), custom_call_target="tpu_custom_call" | custom-call | tf_op jit(solution)/shard_map/pallas_call | solution.py:205
  (1 shorter events, 0.0 us)
Async XLA Ops:
  0.0 3.1 %copy-start = (bf16[128,128]{1,0:T(8,128)(2,1)S(1)}, bf16[128,128]{1,0:T(8,128)(2,1)}, u32[]{:S(2)}) copy-start(bf16[128,128]{1,0:T(8,128)(2,1)} %constant.4.rest_4_) | copy-start | bytes 98308
  0.0 3.1 %copy-start.1 = (bf16[128,128]{1,0:T(8,128)(2,1)S(1)}, bf16[128,128]{1,0:T(8,128)(2,1)}, u32[]{:S(2)}) copy-start(bf16[128,128]{1,0:T(8,128)(2,1)} %constant.2.clone.rest_5_) | copy-start | bytes 98308
  0.0 3.1 %copy-start.2 = (f32[16]{0:T(128)S(1)}, f32[16]{0:T(128)}, u32[]{:S(2)}) copy-start(f32[16]{0:T(128)} %weights.1) | copy-start | bytes 196
  7.5 6.7 %collective-permute-start = (f32[2,5,32,128]{3,2,1,0:T(8,128)S(1)}, f32[2,5,32,128]{3,2,1,0:T(8,128)S(1)}, u32[]{:S(2)}, u32[]{:S(2)}) collective-permute-start(f32[2,5,32,128]{3,2,1,0:T(8,128)S(1)} %get-tuple-element.28), channel_id=1, source_target_pairs={{0,8},{1,9},{2,10},{3,11},{4,12},{5,13},{6,14},{7,15},{8,0},{9,1},... | collective-permute-start | bytes 491528 | tf_op jit(solution)/shard_map/ppermute | solution.py:239
  8.1 15.3 %collective-permute-start.5 = (bf16[16,2,2,32,128]{4,3,2,1,0:T(8,128)(2,1)S(1)}, bf16[16,2,2,32,128]{4,3,2,1,0:T(8,128)(2,1)S(1)}, u32[]{:S(2)}, u32[]{:S(2)}) collective-permute-start(bf16[16,2,2,32,128]{4,3,2,1,0:T(8,128)(2,1)S(1)} %get-tuple-element.24.rest_1_), channel_id=1, source_target_pairs={{0,1},{1,0},{2,3},{3,2},{4,5},{5,4},{6,7},{7,6},{8,9},{9,8},{10,11... | collective-permute-start | bytes 1572872 | tf_op jit(solution)/shard_map/ppermute | solution.py:239
  10.6 15.9 %collective-permute-start.6 = (bf16[16,2,2,32,128]{4,3,2,1,0:T(8,128)(2,1)S(1)}, bf16[16,2,2,32,128]{4,3,2,1,0:T(8,128)(2,1)S(1)}, u32[]{:S(2)}, u32[]{:S(2)}) collective-permute-start(bf16[16,2,2,32,128]{4,3,2,1,0:T(8,128)(2,1)S(1)} %get-tuple-element.23.rest_0_.own), channel_id=1, source_target_pairs={{0,6},{1,3},{2,0},{3,5},{4,2},{5,7},{6,4},{7,1},{8,14},{9,11},{10,... | collective-permute-start | bytes 1572872 | tf_op jit(solution)/shard_map/ppermute | solution.py:239
  14.2 13.5 %collective-permute-start.3 = (bf16[16,2,2,32,128]{4,3,2,1,0:T(8,128)(2,1)S(1)}, bf16[16,2,2,32,128]{4,3,2,1,0:T(8,128)(2,1)S(1)}, u32[]{:S(2)}, u32[]{:S(2)}) collective-permute-start(bf16[16,2,2,32,128]{4,3,2,1,0:T(8,128)(2,1)S(1)} %get-tuple-element.25.rest_2_), channel_id=1, source_target_pairs={{0,8},{1,9},{2,10},{3,11},{4,12},{5,13},{6,14},{7,15},{8,0},{9,1},... | collective-permute-start | bytes 1572872 | tf_op jit(solution)/shard_map/ppermute | solution.py:239
  14.2 19.9 %collective-permute-start.4 = (bf16[16,2,2,32,128]{4,3,2,1,0:T(8,128)(2,1)S(1)}, bf16[16,2,2,32,128]{4,3,2,1,0:T(8,128)(2,1)S(1)}, u32[]{:S(2)}, u32[]{:S(2)}) collective-permute-start(bf16[16,2,2,32,128]{4,3,2,1,0:T(8,128)(2,1)S(1)} %get-tuple-element.26.rest_3_), channel_id=1, source_target_pairs={{0,9},{1,8},{2,11},{3,10},{4,13},{5,12},{6,15},{7,14},{8,1},{9,0},... | collective-permute-start | bytes 1572872 | tf_op jit(solution)/shard_map/ppermute | solution.py:239
  14.2 22.7 %collective-permute-start.8 = (bf16[16,2,2,32,128]{4,3,2,1,0:T(8,128)(2,1)S(1)}, bf16[16,2,2,32,128]{4,3,2,1,0:T(8,128)(2,1)S(1)}, u32[]{:S(2)}, u32[]{:S(2)}) collective-permute-start(bf16[16,2,2,32,128]{4,3,2,1,0:T(8,128)(2,1)S(1)} %get-tuple-element.25.rest_2_), channel_id=1, source_target_pairs={{0,14},{1,11},{2,8},{3,13},{4,10},{5,15},{6,12},{7,9},{8,6},{9,3},... | collective-permute-start | bytes 1572872 | tf_op jit(solution)/shard_map/ppermute | solution.py:239
  23.4 17.0 %collective-permute-start.1 = (f32[5,32,128]{2,1,0:T(8,128)S(1)}, f32[5,32,128]{2,1,0:T(8,128)S(1)}, u32[]{:S(2)}, u32[]{:S(2)}) collective-permute-start(f32[5,32,128]{2,1,0:T(8,128)S(1)} %get-tuple-element.30), channel_id=1, source_target_pairs={{0,16},{1,17},{2,18},{3,19},{4,20},{5,21},{6,22},{7,23},{8,24},{9,... | collective-permute-start | bytes 245768 | tf_op jit(solution)/shard_map/ppermute | solution.py:239
  26.5 1.2 %collective-permute-start.2 = (f32[16,128]{1,0:T(8,128)S(1)}, f32[16,128]{1,0:T(8,128)S(1)}, u32[]{:S(2)}, u32[]{:S(2)}) collective-permute-start(f32[16,128]{1,0:T(8,128)S(1)} %get-tuple-element.31.weights), channel_id=1, source_target_pairs={{0,8},{1,9},{2,10},{3,11},{4,12},{5,13},{6,14},{7,15},{8,0},{9,1},... | collective-permute-start | bytes 24584 | tf_op jit(solution)/shard_map/ppermute | solution.py:239
  34.4 6.0 %collective-permute-start.7 = (f32[2,32,128]{2,1,0:T(8,128)S(1)}, f32[2,32,128]{2,1,0:T(8,128)S(1)}, u32[]{:S(2)}, u32[]{:S(2)}) collective-permute-start(f32[2,32,128]{2,1,0:T(8,128)S(1)} %get-tuple-element.34), channel_id=1, source_target_pairs={{0,16},{1,0},{2,18},{3,2},{4,20},{5,4},{6,22},{7,6},{8,24},{9,8},{... | collective-permute-start | bytes 98312 | tf_op jit(solution)/shard_map/ppermute | solution.py:239
  37.2 4.9 %collective-permute-start.9 = (f32[2,32,128]{2,1,0:T(8,128)S(1)}, f32[2,32,128]{2,1,0:T(8,128)S(1)}, u32[]{:S(2)}, u32[]{:S(2)}) collective-permute-start(f32[2,32,128]{2,1,0:T(8,128)S(1)} %get-tuple-element.37), channel_id=1, source_target_pairs={{0,17},{1,7},{2,19},{3,1},{4,21},{5,3},{6,23},{7,5},{8,25},{9,15},... | collective-permute-start | bytes 98312 | tf_op jit(solution)/shard_map/ppermute | solution.py:239
  38.8 3.9 %collective-permute-start.10 = (f32[2,32,128]{2,1,0:T(8,128)S(1)}, f32[2,32,128]{2,1,0:T(8,128)S(1)}, u32[]{:S(2)}, u32[]{:S(2)}) collective-permute-start(f32[2,32,128]{2,1,0:T(8,128)S(1)} %get-tuple-element.38), channel_id=1, source_target_pairs={{0,18},{1,0},{2,20},{3,2},{4,22},{5,4},{6,16},{7,6},{8,26},{9,8},{... | collective-permute-start | bytes 98312 | tf_op jit(solution)/shard_map/ppermute | solution.py:239
where the time goes:
time: 43.8 us; the launch traced here: 43.4 us
  waiting for transfers between devices  20 us (46%)
  starting transfers between devices  14 us (32%)
  Pallas kernels  9.24 us (21%)
    ppermute x11, waiting for transfers between devices, route(): return lax.ppermute(value, ('band', 'grid'), pairs)  20 us
    ppermute x11, starting transfers between devices, route(): return lax.ppermute(value, ('band', 'grid'), pairs)  14 us
    pallas_call x1, Pallas kernels, lateral(): pl.pallas_call(lateral_kernel, in_specs=[smem] + [vmem] * 6, out_specs=[v...  4.4 us
    pallas_call x2, Pallas kernels, split(): pl.pallas_call(functools.partial(split_kernel, first), in_specs=[pl.Block...  3.07 us
    pallas_call x5, Pallas kernels, call(): pl.pallas_call(kernel, in_specs=[vmem] * len(arrays), out_specs=[vmem] *...  1.77 us
  transfers between devices with their start and end apart: 11, of which 7 were waited for; matrix products, arithmetic and copies ran while one was open for 0% of the time, Pallas kernels for 3%

commit v1 on v0

--- a/solution.py
+++ b/solution.py
@@ -9,7 +9,7 @@
 from jax.sharding import PartitionSpec as P
 
 
-ODD, CORNER, CORE, HALF = range(4, 8)
+ODD, CORNER, CORE, HALF, SWAP = range(4, 9)
 
 
 def stencil(cells):
@@ -76,19 +76,44 @@
     )(weights, *quarters, stencil(nx).T, stencil(ny))
 
 
+def ends():
+    slab = lax.axis_index("grid")
+    levels = lax.axis_size("grid") // 2
+    odd = slab % 2
+    below = slab // 2
+    above = lax.rem(below + 1, levels)
+    leave = jnp.where(odd == 1, above, below)
+    enter = jnp.where(odd == 1, below, above)
+    return any_of(leave, FIRST, levels), any_of(enter, FIRST, levels)
+
+
+def any_of(cycle, members, levels):
+    found = cycle < 0
+    for member in members:
+        found = found | (cycle == member % levels)
+    return found
+
+
 def places():
     odd = lax.axis_index("grid") % 2
     group = lax.axis_index("band")
     core = group % 2
     half = group // 2
+    own = 2 * (1 - odd) + core
+    side = 2 * odd + core
+    sends, _ = ends()
     quarters = (
-        2 * (1 - odd) + core,
-        2 * odd + core,
+        jnp.where(sends, own, side),
+        jnp.where(sends, side, own),
         2 * (1 - odd) + 1 - core,
         2 * odd + 1 - core,
     )
     corner = jnp.where(half == odd, 0, 1)
-    return quarters + (odd, corner, core, half)
+    ahead = corner
+    for slab in CELLS:
+        at = lax.axis_index("grid") == slab % lax.axis_size("grid")
+        ahead = jnp.where(at, 1 - ahead, ahead)
+    return quarters + (odd, corner, core, half, ahead)
 
 
 def split_kernel(first, orbitals, *rest):
@@ -116,7 +141,7 @@
         in_specs=[pl.BlockSpec(memory_space=pltpu.HBM)],
         out_specs=[pl.BlockSpec(memory_space=pltpu.VMEM)] * 3,
         out_shape=[pltpu.VMEM((bands, parts, planes, nx // 4, ny), orbitals.dtype)] * 2
-        + [pltpu.VMEM((8, ny), jnp.int32)],
+        + [pltpu.VMEM((16, ny), jnp.int32)],
         scratch_shapes=[pltpu.SemaphoreType.DMA((2,))],
         compiler_params=pltpu.CompilerParams(vmem_limit_bytes=4 << 20),
         name="split",
@@ -170,13 +195,22 @@
     return (up - sign * low, down - sign * high), (down - sign * low, up - sign * high)
 
 
-def first_kernel(flags, weights, own, side, far, inner, outer):
+def first_kernel(flags, weights, lead, trail, got_lead, got_trail, inner, outer):
     shape = inner.shape[1:]
     odd = flag(flags, ODD, shape)
     zero = (jnp.zeros(shape, jnp.float32),) * 3
-    for out, pair in ((inner, (own, side)), (outer, (side, far))):
-        for i, value in enumerate(edges(odd, weights, *pair, zero)):
-            out[i] = value
+    sends, receives = ends()
+
+    def run(own, side, far):
+        for out, pair in ((inner, (own, side)), (outer, (side, far))):
+            for i, value in enumerate(edges(odd, weights, *pair, zero)):
+                out[i] = value
+
+    for one in (sends, jnp.logical_not(sends)):
+        for two in (receives, jnp.logical_not(receives)):
+            own = lead if one is sends else trail
+            side, far = (got_trail, got_lead) if two is receives else (got_lead, got_trail)
+            pl.when(one & two)(functools.partial(run, own, side, far))
 
 
 def inner_kernel(flags, weights, own, side, sums, kept, near, inner_side):
@@ -195,9 +229,11 @@
     odd = flag(flags, ODD, shape)
     here = flag(flags, CORNER, shape)
     side_parts, far_parts = scaled(odd, edges(odd, weights, side, far, sums))
+    ahead = flag(flags, SWAP, shape)
     for plane in range(2):
-        middle[plane] = jnp.where(here, far_parts[plane], side_parts[plane] + inner_side[plane])
-        distant[plane] = jnp.where(here, side_parts[plane], far_parts[plane])
+        beside = side_parts[plane] + jnp.where(here, 0.0, inner_side[plane])
+        middle[plane] = jnp.where(ahead, beside, far_parts[plane])
+        distant[plane] = jnp.where(ahead, far_parts[plane], beside)
 
 
 def call(kernel, arrays, out_shapes):
@@ -222,7 +258,7 @@
 def per_device(orbitals, occupations):
     slabs = lax.axis_size("grid")
     groups = lax.axis_size("band")
-    assert groups == 4 and slabs % 2 == 0 and orbitals.shape[2] == 2
+    assert groups == 4 and slabs % 2 == 0 and slabs >= 4 and orbitals.shape[2] == 2
 
     def beyond(g):
         return (g + 2) % slabs if g % 2 else (g - 2) % slabs
@@ -238,24 +274,28 @@
                 pairs.append((b * slabs + g, goal[0] * slabs + goal[1]))
         return lax.ppermute(value, ("band", "grid"), pairs)
 
-    own, side, flags = split(0, orbitals)
+    lead, trail, flags = split(0, orbitals)
     own_across, side_across, _ = split(2, orbitals)
 
-    side1 = route(side, lambda b, g: (b, g ^ 1))
-    far1 = route(own, lambda b, g: (b, beyond(g)))
+    def at_end(g):
+        levels = slabs // 2
+        return (g // 2 + g % 2) % levels in [member % levels for member in FIRST]
+
+    got_lead = route(lead, lambda b, g: (b, beyond(g) if at_end(g) else g ^ 1))
+    got_trail = route(trail, lambda b, g: (b, g ^ 1 if at_end(g) else beyond(g)))
     side2 = route(side_across, lambda b, g: (b ^ 1, g ^ 1))
     far2 = route(own_across, lambda b, g: (b ^ 1, beyond(g)))
     own2 = route(own_across, lambda b, g: (b ^ 1, g))
 
-    plane = own.shape[-2:]
-    mine, sent, spread = lateral((own, side, own_across, side_across), occupations)
+    plane = lead.shape[-2:]
+    mine, sent, spread = lateral((lead, trail, own_across, side_across), occupations)
     w2 = route(spread, lambda b, g: (b ^ 1, g))
     theirs = route(sent, lambda b, g: (b ^ 1, g))
     flat, sent = call(halve_kernel, (flags, mine, theirs), [(5,) + plane] * 2)
     flat_rest = route(sent, lambda b, g: (b ^ 2, g))
 
     inner, outer = call(
-        first_kernel, (flags, spread, own, side1, far1), [(3,) + plane] * 2
+        first_kernel, (flags, spread, lead, trail, got_lead, got_trail), [(3,) + plane] * 2
     )
     kept, near, inner_side = call(inner_kernel, (flags, w2, own2, side2, inner), [(2,) + plane] * 3)
 
@@ -266,14 +306,28 @@
     middle, distant = call(
         outer_kernel, (flags, w2, side2, far2, outer, inner_side), [(2,) + plane] * 2
     )
-    got_middle = route(middle, lambda b, g: (b, home(g)) if is_corner(b, g) else (b ^ 2, g ^ 1))
-    got_distant = route(distant, lambda b, g: (b, g ^ 1) if is_corner(b, g) else (b ^ 2, home(g)))
+
+    def beside(b, g):
+        return (b, g ^ 1) if is_corner(b, g) else (b ^ 2, g ^ 1)
+
+    def upward(b, g):
+        return (b, home(g)) if is_corner(b, g) else (b ^ 2, home(g))
+
+    def ahead(b, g):
+        return is_corner(b, g) != (g in [slab % slabs for slab in CELLS])
+
+    got_middle = route(middle, lambda b, g: beside(b, g) if ahead(b, g) else upward(b, g))
+    got_distant = route(distant, lambda b, g: upward(b, g) if ahead(b, g) else beside(b, g))
     arrays = (flat, flat_rest, kept, got_near, got_middle, got_distant)
     (out,) = call(finish_kernel, arrays, [(3, 2) + plane])
     return out
 
 
+FIRST = (-1,)
+CELLS = (1, -1)
 UNROLL = 4
+FIRST = (-1,)
+CELLS = (1, -1)
 
 
 def solution(mesh):

time: 43.8 us -> 43.5 us (level)
  transfers between devices with their start and end apart: 11 -> 11, of which waited for: 7 -> 6; matrix products, arithmetic and copies ran while one was open for 0% -> 0% of each run, Pallas kernels for 3% -> 3%
where the time goes in v1:
time: 43.5 us; the launch traced here: 43.4 us
  waiting for transfers between devices  20 us (46%)
  starting transfers between devices  14 us (32%)
  Pallas kernels  9.25 us (21%)
    ppermute x11, waiting for transfers between devices, route(): return lax.ppermute(value, ('band', 'grid'), pairs)  20 us
    ppermute x11, starting transfers between devices, route(): return lax.ppermute(value, ('band', 'grid'), pairs)  14 us
    pallas_call x1, Pallas kernels, lateral(): pl.pallas_call(lateral_kernel, in_specs=[smem] + [vmem] * 6, out_specs=[v...  4.41 us
    pallas_call x2, Pallas kernels, split(): pl.pallas_call(functools.partial(split_kernel, first), in_specs=[pl.Block...  3.1 us
    pallas_call x5, Pallas kernels, call(): pl.pallas_call(kernel, in_specs=[vmem] * len(arrays), out_specs=[vmem] *...  1.74 us
  transfers between devices with their start and end apart: 11, of which 6 were waited for; matrix products, arithmetic and copies ran while one was open for 0% of the time, Pallas kernels for 3%

profile of v1, /device:TPU:0, one launch (start us, length us, event | category | flops | bytes accessed | tf_op | source)
XLA Modules:
  0.0 43.4 jit_solution(7733013686546835569)
XLA Ops:
  0.0 0.0 copy-start
  0.0 0.0 copy-start.1
  0.0 0.0 copy-start.2
  0.0 1.3 %split.2 = (bf16[16,2,2,32,128]{4,3,2,1,0:T(8,128)(2,1)S(1)}, bf16[16,2,2,32,128]{4,3,2,1,0:T(8,128)(2,1)S(1)}, s32[16,128]{1,0:T(8,128)S(1)}) custom-call(bf16[16,2,2,128,128]{4,3,2,1,0:T(8,128)(2,1)} %orbitals.3), custom_call_target="tpu_custom_call" | custom-call | tf_op jit(solution)/shard_map/split/pallas_call | solution.py:139
  1.3 1.8 %split.3 = (bf16[16,2,2,32,128]{4,3,2,1,0:T(8,128)(2,1)S(1)}, bf16[16,2,2,32,128]{4,3,2,1,0:T(8,128)(2,1)S(1)}, s32[16,128]{1,0:T(8,128)}) custom-call(bf16[16,2,2,128,128]{4,3,2,1,0:T(8,128)(2,1)} %orbitals.3), custom_call_target="tpu_custom_call" | custom-call | tf_op jit(solution)/shard_map/split/pallas_call | solution.py:139
  3.1 0.0 copy-done
  3.1 0.0 copy-done.1
  3.1 0.0 copy-done.2
  3.2 4.4 %lateral.1 = (f32[2,5,32,128]{3,2,1,0:T(8,128)S(1)}, f32[2,5,32,128]{3,2,1,0:T(8,128)S(1)}, f32[16,128]{1,0:T(8,128)S(1)}) custom-call(f32[16]{0:T(128)S(1)} %copy-done.2, bf16[16,2,2,32,128]{4,3,2,1,0:T(8,128)(2,1)S(1)} %get-tuple-element.23.rest_0_.lead, bf16[16,2,2,32,128]{4,3,2,1,0:T(8,128)(2,1)S(1)} %get-tuple-element.24.rest_1_.trail, ...), custom_call_target="tpu_custom_call" | custom-call | tf_op jit(solution)/shard_map/lateral/pallas_call | solution.py:64
  7.6 0.5 %collective-permute-start = (f32[2,5,32,128]{3,2,1,0:T(8,128)S(1)}, f32[2,5,32,128]{3,2,1,0:T(8,128)S(1)}, u32[]{:S(2)}, u32[]{:S(2)}) collective-permute-start(f32[2,5,32,128]{3,2,1,0:T(8,128)S(1)} %get-tuple-element.28), channel_id=1, source_target_pairs={{0,8},{1,9},{2,10},{3,11},{4,12},{5,13},{6,14},{7,15},{8,0},{9,1},... | collective-permute-start | bytes 491528 | tf_op jit(solution)/shard_map/ppermute | solution.py:275
  8.1 2.5 %collective-permute-start.5 = (bf16[16,2,2,32,128]{4,3,2,1,0:T(8,128)(2,1)S(1)}, bf16[16,2,2,32,128]{4,3,2,1,0:T(8,128)(2,1)S(1)}, u32[]{:S(2)}, u32[]{:S(2)}) collective-permute-start(bf16[16,2,2,32,128]{4,3,2,1,0:T(8,128)(2,1)S(1)} %get-tuple-element.23.rest_0_.lead), channel_id=1, source_target_pairs={{0,1},{1,0},{2,3},{3,2},{4,5},{5,7},{6,4},{7,6},{8,9},{9,8},{10,11... | collective-permute-start | bytes 1572872 | tf_op jit(solution)/shard_map/ppermute | solution.py:275
  10.6 2.6 %collective-permute-start.6 = (bf16[16,2,2,32,128]{4,3,2,1,0:T(8,128)(2,1)S(1)}, bf16[16,2,2,32,128]{4,3,2,1,0:T(8,128)(2,1)S(1)}, u32[]{:S(2)}, u32[]{:S(2)}) collective-permute-start(bf16[16,2,2,32,128]{4,3,2,1,0:T(8,128)(2,1)S(1)} %get-tuple-element.24.rest_1_.trail), channel_id=1, source_target_pairs={{0,6},{1,3},{2,0},{3,5},{4,2},{5,4},{6,7},{7,1},{8,14},{9,11},{10,... | collective-permute-start | bytes 1572872 | tf_op jit(solution)/shard_map/ppermute | solution.py:275
  13.2 0.0 collective-permute-start.4
  13.3 0.0 collective-permute-start.3
  13.3 0.0 collective-permute-done.theirs
  13.3 1.7 %collective-permute-start.8 = (bf16[16,2,2,32,128]{4,3,2,1,0:T(8,128)(2,1)S(1)}, bf16[16,2,2,32,128]{4,3,2,1,0:T(8,128)(2,1)S(1)}, u32[]{:S(2)}, u32[]{:S(2)}) collective-permute-start(bf16[16,2,2,32,128]{4,3,2,1,0:T(8,128)(2,1)S(1)} %get-tuple-element.25.rest_2_), channel_id=1, source_target_pairs={{0,14},{1,11},{2,8},{3,13},{4,10},{5,15},{6,12},{7,9},{8,6},{9,3},... | collective-permute-start | bytes 1572872 | tf_op jit(solution)/shard_map/ppermute | solution.py:275
  15.0 8.4 %collective-permute-done.5.got_lead = bf16[16,2,2,32,128]{4,3,2,1,0:T(8,128)(2,1)S(1)} collective-permute-done((bf16[16,2,2,32,128]{4,3,2,1,0:T(8,128)(2,1)S(1)}, bf16[16,2,2,32,128]{4,3,2,1,0:T(8,128)(2,1)S(1)}, u32[]{:S(2)}, u32[]{:S(2)}) %collective-permute-start.5) | collective-permute-done | bytes 524320 | tf_op jit(solution)/shard_map/ppermute | solution.py:275
  23.4 2.1 %collective-permute-start.1 = (f32[5,32,128]{2,1,0:T(8,128)S(1)}, f32[5,32,128]{2,1,0:T(8,128)S(1)}, u32[]{:S(2)}, u32[]{:S(2)}) collective-permute-start(f32[5,32,128]{2,1,0:T(8,128)S(1)} %get-tuple-element.30), channel_id=1, source_target_pairs={{0,16},{1,17},{2,18},{3,19},{4,20},{5,21},{6,22},{7,23},{8,24},{9,... | collective-permute-start | bytes 245768 | tf_op jit(solution)/shard_map/ppermute | solution.py:275
  25.5 0.1 collective-permute-done.6.got_trail
  25.6 0.0 collective-permute-start.2
  25.6 0.5 %shard_map.47 = (f32[3,32,128]{2,1,0:T(8,128)S(1)}, f32[3,32,128]{2,1,0:T(8,128)S(1)}) custom-call(s32[16,128]{1,0:T(8,128)S(1)} %get-tuple-element.22.flags, f32[16,128]{1,0:T(8,128)S(1)} %get-tuple-element.31.weights, bf16[16,2,2,32,128]{4,3,2,1,0:T(8,128)(2,1)S(1)} %get-tuple-element.23.rest_0_.lead, ...), custom_call_target="tpu_custom_call" | custom-call | tf_op jit(solution)/shard_map/pallas_call | solution.py:241
  26.1 0.6 %collective-permute-done.2.weights = f32[16,128]{1,0:T(8,128)S(1)} collective-permute-done((f32[16,128]{1,0:T(8,128)S(1)}, f32[16,128]{1,0:T(8,128)S(1)}, u32[]{:S(2)}, u32[]{:S(2)}) %collective-permute-start.2) | collective-permute-done | bytes 8224 | tf_op jit(solution)/shard_map/ppermute | solution.py:275
  26.7 7.4 %collective-permute-done.4.side = bf16[16,2,2,32,128]{4,3,2,1,0:T(8,128)(2,1)S(1)} collective-permute-done((bf16[16,2,2,32,128]{4,3,2,1,0:T(8,128)(2,1)S(1)}, bf16[16,2,2,32,128]{4,3,2,1,0:T(8,128)(2,1)S(1)}, u32[]{:S(2)}, u32[]{:S(2)}) %collective-permute-start.4) | collective-permute-done | bytes 524320 | tf_op jit(solution)/shard_map/ppermute | solution.py:275
  34.2 0.0 collective-permute-done.3.own
  34.2 0.3 shard_map.48
  34.4 1.6 %collective-permute-start.7 = (f32[2,32,128]{2,1,0:T(8,128)S(1)}, f32[2,32,128]{2,1,0:T(8,128)S(1)}, u32[]{:S(2)}, u32[]{:S(2)}) collective-permute-start(f32[2,32,128]{2,1,0:T(8,128)S(1)} %get-tuple-element.34), channel_id=1, source_target_pairs={{0,16},{1,0},{2,18},{3,2},{4,20},{5,4},{6,22},{7,6},{8,24},{9,8},{... | collective-permute-start | bytes 98312 | tf_op jit(solution)/shard_map/ppermute | solution.py:275
  36.0 0.0 collective-permute-done.8.far
  36.0 0.3 shard_map.49
  36.3 2.5 %collective-permute-start.9 = (f32[2,32,128]{2,1,0:T(8,128)S(1)}, f32[2,32,128]{2,1,0:T(8,128)S(1)}, u32[]{:S(2)}, u32[]{:S(2)}) collective-permute-start(f32[2,32,128]{2,1,0:T(8,128)S(1)} %get-tuple-element.37), channel_id=1, source_target_pairs={{0,18},{1,7},{2,20},{3,2},{4,22},{5,4},{6,16},{7,5},{8,26},{9,15},... | collective-permute-start | bytes 98312 | tf_op jit(solution)/shard_map/ppermute | solution.py:275
  38.8 0.5 %collective-permute-start.10 = (f32[2,32,128]{2,1,0:T(8,128)S(1)}, f32[2,32,128]{2,1,0:T(8,128)S(1)}, u32[]{:S(2)}, u32[]{:S(2)}) collective-permute-start(f32[2,32,128]{2,1,0:T(8,128)S(1)} %get-tuple-element.38), channel_id=1, source_target_pairs={{0,17},{1,0},{2,19},{3,1},{4,21},{5,3},{6,23},{7,6},{8,25},{9,8},{... | collective-permute-start | bytes 98312 | tf_op jit(solution)/shard_map/ppermute | solution.py:275
  39.3 0.0 collective-permute-done.1.flat_rest
  39.3 0.0 collective-permute-done.7.near
  39.3 1.9 %collective-permute-done.9.middle = f32[2,32,128]{2,1,0:T(8,128)S(1)} collective-permute-done((f32[2,32,128]{2,1,0:T(8,128)S(1)}, f32[2,32,128]{2,1,0:T(8,128)S(1)}, u32[]{:S(2)}, u32[]{:S(2)}) %collective-permute-start.9) | collective-permute-done | bytes 32800 | tf_op jit(solution)/shard_map/ppermute | solution.py:275
  41.2 1.6 %collective-permute-done.10.distant = f32[2,32,128]{2,1,0:T(8,128)S(1)} collective-permute-done((f32[2,32,128]{2,1,0:T(8,128)S(1)}, f32[2,32,128]{2,1,0:T(8,128)S(1)}, u32[]{:S(2)}, u32[]{:S(2)}) %collective-permute-start.10) | collective-permute-done | bytes 32800 | tf_op jit(solution)/shard_map/ppermute | solution.py:275
  42.7 0.7 %shard_map.50 = f32[3,2,32,128]{3,2,1,0:T(8,128)} custom-call(f32[5,32,128]{2,1,0:T(8,128)S(1)} %get-tuple-element.29.flat, f32[5,32,128]{2,1,0:T(8,128)S(1)} %collective-permute-done.1.flat_rest, f32[2,32,128]{2,1,0:T(8,128)S(1)} %get-tuple-element.33.kept, f32[2,32,128]{2,1,0:T(8,128)S(1)} %collective-permute-done.7.near, ...), custom_call_target="tpu_custom_call" | custom-call | tf_op jit(solution)/shard_map/pallas_call | solution.py:241
  (1 shorter events, 0.0 us)
Async XLA Ops:
  0.0 3.1 %copy-start = (bf16[128,128]{1,0:T(8,128)(2,1)S(1)}, bf16[128,128]{1,0:T(8,128)(2,1)}, u32[]{:S(2)}) copy-start(bf16[128,128]{1,0:T(8,128)(2,1)} %constant.4.rest_4_) | copy-start | bytes 98308
  0.0 3.1 %copy-start.1 = (bf16[128,128]{1,0:T(8,128)(2,1)S(1)}, bf16[128,128]{1,0:T(8,128)(2,1)}, u32[]{:S(2)}) copy-start(bf16[128,128]{1,0:T(8,128)(2,1)} %constant.2.clone.rest_5_) | copy-start | bytes 98308
  0.0 3.1 %copy-start.2 = (f32[16]{0:T(128)S(1)}, f32[16]{0:T(128)}, u32[]{:S(2)}) copy-start(f32[16]{0:T(128)} %weights.1) | copy-start | bytes 196
  7.6 5.7 %collective-permute-start = (f32[2,5,32,128]{3,2,1,0:T(8,128)S(1)}, f32[2,5,32,128]{3,2,1,0:T(8,128)S(1)}, u32[]{:S(2)}, u32[]{:S(2)}) collective-permute-start(f32[2,5,32,128]{3,2,1,0:T(8,128)S(1)} %get-tuple-element.28), channel_id=1, source_target_pairs={{0,8},{1,9},{2,10},{3,11},{4,12},{5,13},{6,14},{7,15},{8,0},{9,1},... | collective-permute-start | bytes 491528 | tf_op jit(solution)/shard_map/ppermute | solution.py:275
  8.1 15.3 %collective-permute-start.5 = (bf16[16,2,2,32,128]{4,3,2,1,0:T(8,128)(2,1)S(1)}, bf16[16,2,2,32,128]{4,3,2,1,0:T(8,128)(2,1)S(1)}, u32[]{:S(2)}, u32[]{:S(2)}) collective-permute-start(bf16[16,2,2,32,128]{4,3,2,1,0:T(8,128)(2,1)S(1)} %get-tuple-element.23.rest_0_.lead), channel_id=1, source_target_pairs={{0,1},{1,0},{2,3},{3,2},{4,5},{5,7},{6,4},{7,6},{8,9},{9,8},{10,11... | collective-permute-start | bytes 1572872 | tf_op jit(solution)/shard_map/ppermute | solution.py:275
  10.6 14.9 %collective-permute-start.6 = (bf16[16,2,2,32,128]{4,3,2,1,0:T(8,128)(2,1)S(1)}, bf16[16,2,2,32,128]{4,3,2,1,0:T(8,128)(2,1)S(1)}, u32[]{:S(2)}, u32[]{:S(2)}) collective-permute-start(bf16[16,2,2,32,128]{4,3,2,1,0:T(8,128)(2,1)S(1)} %get-tuple-element.24.rest_1_.trail), channel_id=1, source_target_pairs={{0,6},{1,3},{2,0},{3,5},{4,2},{5,4},{6,7},{7,1},{8,14},{9,11},{10,... | collective-permute-start | bytes 1572872 | tf_op jit(solution)/shard_map/ppermute | solution.py:275
  13.2 20.9 %collective-permute-start.4 = (bf16[16,2,2,32,128]{4,3,2,1,0:T(8,128)(2,1)S(1)}, bf16[16,2,2,32,128]{4,3,2,1,0:T(8,128)(2,1)S(1)}, u32[]{:S(2)}, u32[]{:S(2)}) collective-permute-start(bf16[16,2,2,32,128]{4,3,2,1,0:T(8,128)(2,1)S(1)} %get-tuple-element.26.rest_3_), channel_id=1, source_target_pairs={{0,9},{1,8},{2,11},{3,10},{4,13},{5,12},{6,15},{7,14},{8,1},{9,0},... | collective-permute-start | bytes 1572872 | tf_op jit(solution)/shard_map/ppermute | solution.py:275
  13.3 20.9 %collective-permute-start.3 = (bf16[16,2,2,32,128]{4,3,2,1,0:T(8,128)(2,1)S(1)}, bf16[16,2,2,32,128]{4,3,2,1,0:T(8,128)(2,1)S(1)}, u32[]{:S(2)}, u32[]{:S(2)}) collective-permute-start(bf16[16,2,2,32,128]{4,3,2,1,0:T(8,128)(2,1)S(1)} %get-tuple-element.25.rest_2_), channel_id=1, source_target_pairs={{0,8},{1,9},{2,10},{3,11},{4,12},{5,13},{6,14},{7,15},{8,0},{9,1},... | collective-permute-start | bytes 1572872 | tf_op jit(solution)/shard_map/ppermute | solution.py:275
  13.3 22.8 %collective-permute-start.8 = (bf16[16,2,2,32,128]{4,3,2,1,0:T(8,128)(2,1)S(1)}, bf16[16,2,2,32,128]{4,3,2,1,0:T(8,128)(2,1)S(1)}, u32[]{:S(2)}, u32[]{:S(2)}) collective-permute-start(bf16[16,2,2,32,128]{4,3,2,1,0:T(8,128)(2,1)S(1)} %get-tuple-element.25.rest_2_), channel_id=1, source_target_pairs={{0,14},{1,11},{2,8},{3,13},{4,10},{5,15},{6,12},{7,9},{8,6},{9,3},... | collective-permute-start | bytes 1572872 | tf_op jit(solution)/shard_map/ppermute | solution.py:275
  23.4 15.9 %collective-permute-start.1 = (f32[5,32,128]{2,1,0:T(8,128)S(1)}, f32[5,32,128]{2,1,0:T(8,128)S(1)}, u32[]{:S(2)}, u32[]{:S(2)}) collective-permute-start(f32[5,32,128]{2,1,0:T(8,128)S(1)} %get-tuple-element.30), channel_id=1, source_target_pairs={{0,16},{1,17},{2,18},{3,19},{4,20},{5,21},{6,22},{7,23},{8,24},{9,... | collective-permute-start | bytes 245768 | tf_op jit(solution)/shard_map/ppermute | solution.py:275
  25.6 1.2 %collective-permute-start.2 = (f32[16,128]{1,0:T(8,128)S(1)}, f32[16,128]{1,0:T(8,128)S(1)}, u32[]{:S(2)}, u32[]{:S(2)}) collective-permute-start(f32[16,128]{1,0:T(8,128)S(1)} %get-tuple-element.31.weights), channel_id=1, source_target_pairs={{0,8},{1,9},{2,10},{3,11},{4,12},{5,13},{6,14},{7,15},{8,0},{9,1},... | collective-permute-start | bytes 24584 | tf_op jit(solution)/shard_map/ppermute | solution.py:275
  34.4 4.8 %collective-permute-start.7 = (f32[2,32,128]{2,1,0:T(8,128)S(1)}, f32[2,32,128]{2,1,0:T(8,128)S(1)}, u32[]{:S(2)}, u32[]{:S(2)}) collective-permute-start(f32[2,32,128]{2,1,0:T(8,128)S(1)} %get-tuple-element.34), channel_id=1, source_target_pairs={{0,16},{1,0},{2,18},{3,2},{4,20},{5,4},{6,22},{7,6},{8,24},{9,8},{... | collective-permute-start | bytes 98312 | tf_op jit(solution)/shard_map/ppermute | solution.py:275
  36.3 4.9 %collective-permute-start.9 = (f32[2,32,128]{2,1,0:T(8,128)S(1)}, f32[2,32,128]{2,1,0:T(8,128)S(1)}, u32[]{:S(2)}, u32[]{:S(2)}) collective-permute-start(f32[2,32,128]{2,1,0:T(8,128)S(1)} %get-tuple-element.37), channel_id=1, source_target_pairs={{0,18},{1,7},{2,20},{3,2},{4,22},{5,4},{6,16},{7,5},{8,26},{9,15},... | collective-permute-start | bytes 98312 | tf_op jit(solution)/shard_map/ppermute | solution.py:275
  38.8 3.9 %collective-permute-start.10 = (f32[2,32,128]{2,1,0:T(8,128)S(1)}, f32[2,32,128]{2,1,0:T(8,128)S(1)}, u32[]{:S(2)}, u32[]{:S(2)}) collective-permute-start(f32[2,32,128]{2,1,0:T(8,128)S(1)} %get-tuple-element.38), channel_id=1, source_target_pairs={{0,17},{1,0},{2,19},{3,1},{4,21},{5,3},{6,23},{7,6},{8,25},{9,8},{... | collective-permute-start | bytes 98312 | tf_op jit(solution)/shard_map/ppermute | solution.py:275

commit v2 on v1

--- a/solution.py
+++ b/solution.py
@@ -9,7 +9,7 @@
 from jax.sharding import PartitionSpec as P
 
 
-ODD, CORNER, CORE, HALF, SWAP = range(4, 9)
+ODD, CORNER, CORE, HALF, SWAP, OWN, SIDE = range(4, 11)
 
 
 def stencil(cells):
@@ -19,20 +19,23 @@
     return jnp.asarray(8.0 * near - far, jnp.bfloat16)
 
 
-def lateral_kernel(weights, *rest):
-    quarters, (across, along, kept, sent, spread, field, total) = rest[:4], rest[4:]
-    bands, parts, planes, rows, _ = quarters[0].shape
+def lateral_kernel(pieces, weights, *rest):
+    count = len(pieces)
+    arrays, (across, along, kept, sent, spread, field, total) = rest[:count], rest[count:]
+    _, parts, planes, rows, _ = arrays[0].shape
+    bands = max(stop for _, _, stop in pieces)
     table = places()
     total[...] = jnp.zeros_like(total)
     dot = functools.partial(jnp.dot, preferred_element_type=jnp.float32)
 
-    def advance(n, carry):
+    def advance(start, stop, n, carry):
         weight = weights[n]
-        for i, quarter in enumerate(quarters):
-            at = pl.ds(pl.multiple_of(table[i] * rows, rows), rows)
-            for part in range(parts):
-                for plane in range(planes):
-                    field[part, plane, at] = quarter[n, part, plane]
+        for array, (quarter, low, high) in zip(arrays, pieces):
+            if low <= start and stop <= high:
+                at = pl.ds(pl.multiple_of(table[quarter] * rows, rows), rows)
+                for part in range(parts):
+                    for plane in range(planes):
+                        field[part, plane, at] = array[n - low, part, plane]
         fields = []
         for plane in range(planes):
             re16 = field[0, plane]
@@ -46,7 +49,9 @@
         total[0] += 8.0 * (re * im_up.astype(jnp.float32) - im * re_up.astype(jnp.float32))
         return carry
 
-    lax.fori_loop(0, bands, advance, 0)
+    cuts = sorted({cut for _, low, high in pieces for cut in (low, high)})
+    for start, stop in zip(cuts, cuts[1:]):
+        lax.fori_loop(start, stop, functools.partial(advance, start, stop), 0)
     for n in range(bands):
         spread[n : n + 1] = jnp.full((1, spread.shape[1]), weights[n], jnp.float32)
     core = table[CORE]
@@ -56,24 +61,24 @@
             out[half] = total[:, at] * (1.0 / 12.0)
 
 
-def lateral(quarters, weights):
-    bands, parts, planes, rows, ny = quarters[0].shape
+def lateral(pieces, arrays, weights):
+    _, parts, planes, rows, ny = arrays[0].shape
     nx = 4 * rows
     smem = pl.BlockSpec(memory_space=pltpu.SMEM)
     vmem = pl.BlockSpec(memory_space=pltpu.VMEM)
     return pl.pallas_call(
-        lateral_kernel,
-        in_specs=[smem] + [vmem] * 6,
+        functools.partial(lateral_kernel, pieces),
+        in_specs=[smem] + [vmem] * (len(arrays) + 2),
         out_specs=[vmem] * 3,
         out_shape=[jax.ShapeDtypeStruct((2, 5, rows, ny), jnp.float32)] * 2
-        + [jax.ShapeDtypeStruct((bands, ny), jnp.float32)],
+        + [jax.ShapeDtypeStruct(weights.shape + (ny,), jnp.float32)],
         scratch_shapes=[
-            pltpu.VMEM((parts, planes, nx, ny), quarters[0].dtype),
+            pltpu.VMEM((parts, planes, nx, ny), arrays[0].dtype),
             pltpu.VMEM((5, nx, ny), jnp.float32),
         ],
         compiler_params=pltpu.CompilerParams(vmem_limit_bytes=8 << 20),
         name="lateral",
-    )(weights, *quarters, stencil(nx).T, stencil(ny))
+    )(weights, *arrays, stencil(nx).T, stencil(ny))
 
 
 def ends():
@@ -113,18 +118,22 @@
     for slab in CELLS:
         at = lax.axis_index("grid") == slab % lax.axis_size("grid")
         ahead = jnp.where(at, 1 - ahead, ahead)
-    return quarters + (odd, corner, core, half, ahead)
-
-
-def split_kernel(first, orbitals, *rest):
-    outs, flags, sem = rest[:2], rest[2], rest[3]
+    return quarters + (odd, corner, core, half, ahead, own, side)
+
+
+def split_kernel(pieces, orbitals, *rest):
+    outs, flags, sem = rest[:-2], rest[-2], rest[-1]
     rows = outs[0].shape[3]
     table = places()
     copies = [
         pltpu.make_async_copy(
-            orbitals.at[:, :, :, pl.ds(pl.multiple_of(table[first + i] * rows, rows), rows)], out, sem.at[i]
+            orbitals.at[
+                low:high, :, :, pl.ds(pl.multiple_of(table[quarter] * rows, rows), rows)
+            ],
+            out,
+            sem.at[i],
         )
-        for i, out in enumerate(outs)
+        for i, (out, (quarter, low, high)) in enumerate(zip(outs, pieces))
     ]
     for copy in copies:
         copy.start()
@@ -134,15 +143,19 @@
         copy.wait()
 
 
-def split(first, orbitals):
-    bands, parts, planes, nx, ny = orbitals.shape
+def split(pieces, orbitals):
+    _, parts, planes, nx, ny = orbitals.shape
+    count = len(pieces)
     return pl.pallas_call(
-        functools.partial(split_kernel, first),
+        functools.partial(split_kernel, pieces),
         in_specs=[pl.BlockSpec(memory_space=pltpu.HBM)],
-        out_specs=[pl.BlockSpec(memory_space=pltpu.VMEM)] * 3,
-        out_shape=[pltpu.VMEM((bands, parts, planes, nx // 4, ny), orbitals.dtype)] * 2
+        out_specs=[pl.BlockSpec(memory_space=pltpu.VMEM)] * (count + 1),
+        out_shape=[
+            pltpu.VMEM((high - low, parts, planes, nx // 4, ny), orbitals.dtype)
+            for _, low, high in pieces
+        ]
         + [pltpu.VMEM((16, ny), jnp.int32)],
-        scratch_shapes=[pltpu.SemaphoreType.DMA((2,))],
+        scratch_shapes=[pltpu.SemaphoreType.DMA((count,))],
         compiler_params=pltpu.CompilerParams(vmem_limit_bytes=4 << 20),
         name="split",
     )(pltpu.with_memory_space_constraint(orbitals, pltpu.HBM))
@@ -157,7 +170,7 @@
         sent[i] = jnp.where(lower, high, low)
 
 
-def edges(odd, weights, first, second, sums):
+def edges(weights, offset, first, second, sums):
     def advance(n, sums):
         def field(rows, scale=None):
             values = [[rows[n, part, k].astype(jnp.float32) for part in range(2)] for k in range(2)]
@@ -165,21 +178,14 @@
                 values = [[scale * value for value in plane] for plane in values]
             return values
 
-        def pick(low, high):
-            return [jnp.where(odd, a, b) for a, b in zip(low, high)]
-
         def term(low, high):
             return low[0] * high[1] - low[1] * high[0]
 
-        f, g = field(first, weights[pl.ds(n, 1)]), field(second)
-        new = (
-            term(f[0], g[0]),
-            term(f[1], g[1]),
-            term(pick(f[0], f[1]), pick(g[1], g[0])),
-        )
-        return tuple(a + b for a, b in zip(sums, new))
-
-    sums = tuple(sums[i] for i in range(3))
+        f, g = field(first, weights[pl.ds(n + offset, 1)]), field(second)
+        pairs = ((0, 0), (1, 1), (1, 0), (0, 1))
+        return tuple(old + term(f[low], g[high]) for old, (low, high) in zip(sums, pairs))
+
+    sums = tuple(sums[i] for i in range(4))
     return lax.fori_loop(0, first.shape[0], advance, sums, unroll=UNROLL)
 
 
@@ -189,46 +195,52 @@
 
 def scaled(odd, sums):
     sign = jnp.where(odd, -1.0 / 12.0, 1.0 / 12.0)
-    low, high, mid = sums
+    low, high, even_mid, odd_mid = sums
+    mid = jnp.where(odd, odd_mid, even_mid)
     up = jnp.where(odd, -8.0 / 12.0, 0.0) * mid
     down = jnp.where(odd, 0.0, 8.0 / 12.0) * mid
     return (up - sign * low, down - sign * high), (down - sign * low, up - sign * high)
 
 
-def first_kernel(flags, weights, lead, trail, got_lead, got_trail, inner, outer):
-    shape = inner.shape[1:]
-    odd = flag(flags, ODD, shape)
-    zero = (jnp.zeros(shape, jnp.float32),) * 3
+def add_edges(weights, offset, own, side, far, inner, outer, before=None):
+    zero = (jnp.zeros(inner.shape[1:], jnp.float32),) * 4
+    for i, (out, pair) in enumerate(((inner, (own, side)), (outer, (side, far)))):
+        start = before[i] if before else zero
+        for j, value in enumerate(edges(weights, offset, *pair, start)):
+            out[j] = value
+
+
+def first_kernel(weights, lead, trail, got_lead, got_trail, own1, side1, far1, inner, outer):
     sends, receives = ends()
-
-    def run(own, side, far):
-        for out, pair in ((inner, (own, side)), (outer, (side, far))):
-            for i, value in enumerate(edges(odd, weights, *pair, zero)):
-                out[i] = value
-
     for one in (sends, jnp.logical_not(sends)):
         for two in (receives, jnp.logical_not(receives)):
             own = lead if one is sends else trail
             side, far = (got_trail, got_lead) if two is receives else (got_lead, got_trail)
-            pl.when(one & two)(functools.partial(run, own, side, far))
-
-
-def inner_kernel(flags, weights, own, side, sums, kept, near, inner_side):
+            run = functools.partial(add_edges, weights, 0, own, side, far, inner, outer)
+            pl.when(one & two)(run)
+    add_edges(weights, lead.shape[0], own1, side1, far1, inner, outer, (inner, outer))
+
+
+def second_kernel(weights, own, side, far, old_inner, old_outer, inner, outer):
+    add_edges(weights, 0, own, side, far, inner, outer, (old_inner, old_outer))
+
+
+def inner_kernel(offset, flags, weights, own, side, sums, kept, near, inner_side):
     shape = kept.shape[1:]
     odd = flag(flags, ODD, shape)
     here = flag(flags, CORNER, shape)
-    own_parts, side_parts = scaled(odd, edges(odd, weights, own, side, sums))
+    own_parts, side_parts = scaled(odd, edges(weights, offset, own, side, sums))
     for plane in range(2):
         kept[plane] = jnp.where(here, own_parts[plane], 0.0)
         near[plane] = jnp.where(here, side_parts[plane], own_parts[plane])
         inner_side[plane] = side_parts[plane]
 
 
-def outer_kernel(flags, weights, side, far, sums, inner_side, middle, distant):
+def outer_kernel(offset, flags, weights, side, far, sums, inner_side, middle, distant):
     shape = middle.shape[1:]
     odd = flag(flags, ODD, shape)
     here = flag(flags, CORNER, shape)
-    side_parts, far_parts = scaled(odd, edges(odd, weights, side, far, sums))
+    side_parts, far_parts = scaled(odd, edges(weights, offset, side, far, sums))
     ahead = flag(flags, SWAP, shape)
     for plane in range(2):
         beside = side_parts[plane] + jnp.where(here, 0.0, inner_side[plane])
@@ -274,8 +286,14 @@
                 pairs.append((b * slabs + g, goal[0] * slabs + goal[1]))
         return lax.ppermute(value, ("band", "grid"), pairs)
 
-    lead, trail, flags = split(0, orbitals)
-    own_across, side_across, _ = split(2, orbitals)
+    bands = orbitals.shape[0]
+    cut = bands * 5 // 8
+    chunks = ((0, cut), (cut, bands), (0, cut), (cut, bands))
+    pieces = [(2 * (k // 2) + part,) + chunk for k, chunk in enumerate(chunks) for part in range(2)]
+    lead, trail, flags = split(pieces[:2], orbitals)
+    pieces[2:4] = [(OWN, cut, bands), (SIDE, cut, bands)]
+    rest = list(split(pieces[2:], orbitals)[:-1])
+    arrays = [lead, trail] + rest
 
     def at_end(g):
         levels = slabs // 2
@@ -283,28 +301,42 @@
 
     got_lead = route(lead, lambda b, g: (b, beyond(g) if at_end(g) else g ^ 1))
     got_trail = route(trail, lambda b, g: (b, g ^ 1 if at_end(g) else beyond(g)))
-    side2 = route(side_across, lambda b, g: (b ^ 1, g ^ 1))
-    far2 = route(own_across, lambda b, g: (b ^ 1, beyond(g)))
-    own2 = route(own_across, lambda b, g: (b ^ 1, g))
+    own, side, far = [None, rest[0], None, None], [None] * 4, [None] * 4
+    for k in range(1, 4):
+        mine, theirs = rest[2 * k - 2 : 2 * k]
+        swap = k // 2
+        side[k] = route(theirs, lambda b, g: (b ^ swap, g ^ 1))
+        far[k] = route(mine, lambda b, g: (b ^ swap, beyond(g)))
+        if swap:
+            own[k] = route(mine, lambda b, g: (b ^ 1, g))
 
     plane = lead.shape[-2:]
-    mine, sent, spread = lateral((lead, trail, own_across, side_across), occupations)
+    mine, sent, spread = lateral(pieces, arrays, occupations)
     w2 = route(spread, lambda b, g: (b ^ 1, g))
     theirs = route(sent, lambda b, g: (b ^ 1, g))
     flat, sent = call(halve_kernel, (flags, mine, theirs), [(5,) + plane] * 2)
     flat_rest = route(sent, lambda b, g: (b ^ 2, g))
 
-    inner, outer = call(
-        first_kernel, (flags, spread, lead, trail, got_lead, got_trail), [(3,) + plane] * 2
-    )
-    kept, near, inner_side = call(inner_kernel, (flags, w2, own2, side2, inner), [(2,) + plane] * 3)
+    sums = call(
+        first_kernel,
+        (spread, lead, trail, got_lead, got_trail, own[1], side[1], far[1]),
+        [(4,) + plane] * 2,
+    )
+    inner, outer = call(second_kernel, (w2, own[2], side[2], far[2], *sums), [(4,) + plane] * 2)
+    kept, near, inner_side = call(
+        functools.partial(inner_kernel, cut),
+        (flags, w2, own[3], side[3], inner),
+        [(2,) + plane] * 3,
+    )
 
     def is_corner(b, g):
         return b // 2 != g % 2
 
     got_near = route(near, lambda b, g: (b, g ^ 1) if is_corner(b, g) else (b ^ 2, g))
     middle, distant = call(
-        outer_kernel, (flags, w2, side2, far2, outer, inner_side), [(2,) + plane] * 2
+        functools.partial(outer_kernel, cut),
+        (flags, w2, side[3], far[3], outer, inner_side),
+        [(2,) + plane] * 2,
     )
 
     def beside(b, g):

time: 43.5 us -> 45.8 us (1.053)
  starting transfers between devices: 14 us -> 17.8 us
  waiting for transfers between devices: 20 us -> 18.3 us
    ppermute x11 -> x16, starting transfers between devices: 14 us -> 17.8 us  [route(): return lax.ppermute(value, ('band', 'grid'), pairs)]
    ppermute x11 -> x16, waiting for transfers between devices: 20 us -> 18.3 us  [route(): return lax.ppermute(value, ('band', 'grid'), pairs)]
    pallas_call x5 -> x6, Pallas kernels: 1.74 us -> 1.83 us  [call(): pl.pallas_call(kernel, in_specs=[vmem] * len(arrays), out_specs=[vmem] *...]
  transfers between devices with their start and end apart: 11 -> 16, of which waited for: 6 -> 6; matrix products, arithmetic and copies ran while one was open for 0% -> 0% of each run, Pallas kernels for 3% -> 3%
where the time goes in v2:
time: 45.8 us; the launch traced here: 45.6 us
  waiting for transfers between devices  18.3 us (40%)
  starting transfers between devices  17.8 us (39%)
  Pallas kernels  9.43 us (21%)
    ppermute x16, waiting for transfers between devices, route(): return lax.ppermute(value, ('band', 'grid'), pairs)  18.3 us
    ppermute x16, starting transfers between devices, route(): return lax.ppermute(value, ('band', 'grid'), pairs)  17.8 us
    pallas_call x1, Pallas kernels, lateral(): pl.pallas_call(functools.partial(lateral_kernel, pieces), in_specs=[smem]...  4.42 us
    pallas_call x2, Pallas kernels, split(): pl.pallas_call(functools.partial(split_kernel, pieces), in_specs=[pl.Bloc...  3.17 us
    pallas_call x6, Pallas kernels, call(): pl.pallas_call(kernel, in_specs=[vmem] * len(arrays), out_specs=[vmem] *...  1.83 us
  transfers between devices with their start and end apart: 16, of which 6 were waited for; matrix products, arithmetic and copies ran while one was open for 0% of the time, Pallas kernels for 3%

profile of v2, /device:TPU:0, one launch (start us, length us, event | category | flops | bytes accessed | tf_op | source)
XLA Modules:
  0.0 45.6 jit_solution(5270744295002120505)
XLA Ops:
  0.0 0.0 copy-start
  0.0 0.0 copy-start.1
  0.0 0.0 copy-start.2
  0.0 2.1 %split.3 = (bf16[6,2,2,32,128]{4,3,2,1,0:T(8,128)(2,1)S(1)}, bf16[6,2,2,32,128]{4,3,2,1,0:T(8,128)(2,1)S(1)}, bf16[10,2,2,32,128]{4,3,2,1,0:T(8,128)(2,1)S(1)}, ...) custom-call(bf16[16,2,2,128,128]{4,3,2,1,0:T(8,128)(2,1)} %orbitals.3), custom_call_target="tpu_custom_call" | custom-call | tf_op jit(solution)/shard_map/split/pallas_call | solution.py:149
  2.1 1.1 %split.2 = (bf16[10,2,2,32,128]{4,3,2,1,0:T(8,128)(2,1)S(1)}, bf16[10,2,2,32,128]{4,3,2,1,0:T(8,128)(2,1)S(1)}, s32[16,128]{1,0:T(8,128)S(1)}) custom-call(bf16[16,2,2,128,128]{4,3,2,1,0:T(8,128)(2,1)} %orbitals.3), custom_call_target="tpu_custom_call" | custom-call | tf_op jit(solution)/shard_map/split/pallas_call | solution.py:149
  3.2 0.0 copy-done
  3.2 0.0 copy-done.1
  3.2 0.0 copy-done.2
  3.2 4.4 %lateral.1 = (f32[2,5,32,128]{3,2,1,0:T(8,128)S(1)}, f32[2,5,32,128]{3,2,1,0:T(8,128)S(1)}, f32[16,128]{1,0:T(8,128)S(1)}) custom-call(f32[16]{0:T(128)S(1)} %copy-done.2, bf16[10,2,2,32,128]{4,3,2,1,0:T(8,128)(2,1)S(1)} %get-tuple-element.29.rest_0_.lead, bf16[10,2,2,32,128]{4,3,2,1,0:T(8,128)(2,1)S(1)} %get-tuple-element.30.rest_1_.trail, ...), custom_call_target="tpu_custom_call" | custom-call | tf_op jit(solution)/shard_map/lateral/pallas_call | solution.py:69
  7.7 0.6 %collective-permute-start = (f32[2,5,32,128]{3,2,1,0:T(8,128)S(1)}, f32[2,5,32,128]{3,2,1,0:T(8,128)S(1)}, u32[]{:S(2)}, u32[]{:S(2)}) collective-permute-start(f32[2,5,32,128]{3,2,1,0:T(8,128)S(1)} %get-tuple-element.38), channel_id=1, source_target_pairs={{0,8},{1,9},{2,10},{3,11},{4,12},{5,13},{6,14},{7,15},{8,0},{9,1},... | collective-permute-start | bytes 491528 | tf_op jit(solution)/shard_map/ppermute | solution.py:287
  8.2 4.7 %collective-permute-start.11 = (bf16[6,2,2,32,128]{4,3,2,1,0:T(8,128)(2,1)S(1)}, bf16[6,2,2,32,128]{4,3,2,1,0:T(8,128)(2,1)S(1)}, u32[]{:S(2)}, u32[]{:S(2)}) collective-permute-start(bf16[6,2,2,32,128]{4,3,2,1,0:T(8,128)(2,1)S(1)} %get-tuple-element.31.rest_2_.own1), channel_id=1, source_target_pairs={{0,6},{1,3},{2,0},{3,5},{4,2},{5,7},{6,4},{7,1},{8,14},{9,11},{10,... | collective-permute-start | bytes 589832 | tf_op jit(solution)/shard_map/ppermute | solution.py:287
  12.9 0.2 collective-permute-start.2
  13.1 0.0 collective-permute-start.10
  13.1 2.0 %collective-permute-start.8 = (bf16[10,2,2,32,128]{4,3,2,1,0:T(8,128)(2,1)S(1)}, bf16[10,2,2,32,128]{4,3,2,1,0:T(8,128)(2,1)S(1)}, u32[]{:S(2)}, u32[]{:S(2)}) collective-permute-start(bf16[10,2,2,32,128]{4,3,2,1,0:T(8,128)(2,1)S(1)} %get-tuple-element.29.rest_0_.lead), channel_id=1, source_target_pairs={{0,1},{1,0},{2,3},{3,2},{4,5},{5,7},{6,4},{7,6},{8,9},{9,8},{10,11... | collective-permute-start | bytes 983048 | tf_op jit(solution)/shard_map/ppermute | solution.py:287
  15.1 0.0 collective-permute-done.2.weights
  15.1 1.5 %collective-permute-start.9 = (bf16[10,2,2,32,128]{4,3,2,1,0:T(8,128)(2,1)S(1)}, bf16[10,2,2,32,128]{4,3,2,1,0:T(8,128)(2,1)S(1)}, u32[]{:S(2)}, u32[]{:S(2)}) collective-permute-start(bf16[10,2,2,32,128]{4,3,2,1,0:T(8,128)(2,1)S(1)} %get-tuple-element.30.rest_1_.trail), channel_id=1, source_target_pairs={{0,6},{1,3},{2,0},{3,5},{4,2},{5,4},{6,7},{7,1},{8,14},{9,11},{10,... | collective-permute-start | bytes 983048 | tf_op jit(solution)/shard_map/ppermute | solution.py:287
  16.5 0.0 collective-permute-done.theirs
  16.5 0.0 collective-permute-start.5
  16.5 1.6 %collective-permute-done.11.far1 = bf16[6,2,2,32,128]{4,3,2,1,0:T(8,128)(2,1)S(1)} collective-permute-done((bf16[6,2,2,32,128]{4,3,2,1,0:T(8,128)(2,1)S(1)}, bf16[6,2,2,32,128]{4,3,2,1,0:T(8,128)(2,1)S(1)}, u32[]{:S(2)}, u32[]{:S(2)}) %collective-permute-start.11) | collective-permute-done | bytes 196640 | tf_op jit(solution)/shard_map/ppermute | solution.py:287
  18.2 3.0 %collective-permute-start.7 = (bf16[10,2,2,32,128]{4,3,2,1,0:T(8,128)(2,1)S(1)}, bf16[10,2,2,32,128]{4,3,2,1,0:T(8,128)(2,1)S(1)}, u32[]{:S(2)}, u32[]{:S(2)}) collective-permute-start(bf16[10,2,2,32,128]{4,3,2,1,0:T(8,128)(2,1)S(1)} %get-tuple-element.33.rest_4_), channel_id=1, source_target_pairs={{0,14},{1,11},{2,8},{3,13},{4,10},{5,15},{6,12},{7,9},{8,6},{9,3},... | collective-permute-start | bytes 983048 | tf_op jit(solution)/shard_map/ppermute | solution.py:287
  21.1 0.0 collective-permute-done.10.side1
  21.1 0.0 collective-permute-start.6
  21.1 6.7 %collective-permute-done.8.got_lead = bf16[10,2,2,32,128]{4,3,2,1,0:T(8,128)(2,1)S(1)} collective-permute-done((bf16[10,2,2,32,128]{4,3,2,1,0:T(8,128)(2,1)S(1)}, bf16[10,2,2,32,128]{4,3,2,1,0:T(8,128)(2,1)S(1)}, u32[]{:S(2)}, u32[]{:S(2)}) %collective-permute-start.8) | collective-permute-done | bytes 327712 | tf_op jit(solution)/shard_map/ppermute | solution.py:287
  27.8 0.0 collective-permute-start.3
  27.9 0.0 collective-permute-done.9.got_trail
  27.9 0.1 collective-permute-start.4
  28.0 0.0 collective-permute-done.5.own
  28.0 1.3 %collective-permute-start.13 = (bf16[6,2,2,32,128]{4,3,2,1,0:T(8,128)(2,1)S(1)}, bf16[6,2,2,32,128]{4,3,2,1,0:T(8,128)(2,1)S(1)}, u32[]{:S(2)}, u32[]{:S(2)}) collective-permute-start(bf16[6,2,2,32,128]{4,3,2,1,0:T(8,128)(2,1)S(1)} %get-tuple-element.35.rest_6_), channel_id=1, source_target_pairs={{0,14},{1,11},{2,8},{3,13},{4,10},{5,15},{6,12},{7,9},{8,6},{9,3},... | collective-permute-start | bytes 589832 | tf_op jit(solution)/shard_map/ppermute | solution.py:287
  29.3 2.9 %collective-permute-done.7.far = bf16[10,2,2,32,128]{4,3,2,1,0:T(8,128)(2,1)S(1)} collective-permute-done((bf16[10,2,2,32,128]{4,3,2,1,0:T(8,128)(2,1)S(1)}, bf16[10,2,2,32,128]{4,3,2,1,0:T(8,128)(2,1)S(1)}, u32[]{:S(2)}, u32[]{:S(2)}) %collective-permute-start.7) | collective-permute-done | bytes 327712 | tf_op jit(solution)/shard_map/ppermute | solution.py:287
  32.2 1.5 %collective-permute-start.1 = (f32[5,32,128]{2,1,0:T(8,128)S(1)}, f32[5,32,128]{2,1,0:T(8,128)S(1)}, u32[]{:S(2)}, u32[]{:S(2)}) collective-permute-start(f32[5,32,128]{2,1,0:T(8,128)S(1)} %get-tuple-element.40), channel_id=1, source_target_pairs={{0,16},{1,17},{2,18},{3,19},{4,20},{5,21},{6,22},{7,23},{8,24},{9,... | collective-permute-start | bytes 245768 | tf_op jit(solution)/shard_map/ppermute | solution.py:287
  33.7 0.6 %shard_map.47 = (f32[4,32,128]{2,1,0:T(8,128)S(1)}, f32[4,32,128]{2,1,0:T(8,128)S(1)}) custom-call(f32[16,128]{1,0:T(8,128)S(1)} %get-tuple-element.41.weights, bf16[10,2,2,32,128]{4,3,2,1,0:T(8,128)(2,1)S(1)} %get-tuple-element.29.rest_0_.lead, bf16[10,2,2,32,128]{4,3,2,1,0:T(8,128)(2,1)S(1)} %get-tuple-element.30.rest_1_.trail, ...), custom_call_target="tpu_custom_call" | custom-call | tf_op jit(solution)/shard_map/pallas_call | solution.py:253
  34.3 0.0 collective-permute-done.6.side
  34.3 0.4 shard_map.48
  34.7 0.0 collective-permute-done.3.own
  34.7 3.2 %collective-permute-done.4.side = bf16[6,2,2,32,128]{4,3,2,1,0:T(8,128)(2,1)S(1)} collective-permute-done((bf16[6,2,2,32,128]{4,3,2,1,0:T(8,128)(2,1)S(1)}, bf16[6,2,2,32,128]{4,3,2,1,0:T(8,128)(2,1)S(1)}, u32[]{:S(2)}, u32[]{:S(2)}) %collective-permute-start.4) | collective-permute-done | bytes 196640 | tf_op jit(solution)/shard_map/ppermute | solution.py:287
  37.8 0.1 shard_map.49
  38.0 0.0 collective-permute-done.13.far
  38.0 0.1 shard_map.50
  38.1 0.6 %collective-permute-start.14 = (f32[2,32,128]{2,1,0:T(8,128)S(1)}, f32[2,32,128]{2,1,0:T(8,128)S(1)}, u32[]{:S(2)}, u32[]{:S(2)}) collective-permute-start(f32[2,32,128]{2,1,0:T(8,128)S(1)} %get-tuple-element.49), channel_id=1, source_target_pairs={{0,18},{1,7},{2,20},{3,2},{4,22},{5,4},{6,16},{7,5},{8,26},{9,15},... | collective-permute-start | bytes 98312 | tf_op jit(solution)/shard_map/ppermute | solution.py:287
  38.6 2.4 %collective-permute-start.15 = (f32[2,32,128]{2,1,0:T(8,128)S(1)}, f32[2,32,128]{2,1,0:T(8,128)S(1)}, u32[]{:S(2)}, u32[]{:S(2)}) collective-permute-start(f32[2,32,128]{2,1,0:T(8,128)S(1)} %get-tuple-element.50), channel_id=1, source_target_pairs={{0,17},{1,0},{2,19},{3,1},{4,21},{5,3},{6,23},{7,6},{8,25},{9,8},{... | collective-permute-start | bytes 98312 | tf_op jit(solution)/shard_map/ppermute | solution.py:287
  41.1 0.0 collective-permute-start.12
  41.1 0.0 collective-permute-done.1.flat_rest
  41.1 1.9 %collective-permute-done.14.middle = f32[2,32,128]{2,1,0:T(8,128)S(1)} collective-permute-done((f32[2,32,128]{2,1,0:T(8,128)S(1)}, f32[2,32,128]{2,1,0:T(8,128)S(1)}, u32[]{:S(2)}, u32[]{:S(2)}) %collective-permute-start.14) | collective-permute-done | bytes 32800 | tf_op jit(solution)/shard_map/ppermute | solution.py:287
  43.0 0.0 collective-permute-done.15.distant
  43.0 2.0 %collective-permute-done.12.near = f32[2,32,128]{2,1,0:T(8,128)S(1)} collective-permute-done((f32[2,32,128]{2,1,0:T(8,128)S(1)}, f32[2,32,128]{2,1,0:T(8,128)S(1)}, u32[]{:S(2)}, u32[]{:S(2)}) %collective-permute-start.12) | collective-permute-done | bytes 32800 | tf_op jit(solution)/shard_map/ppermute | solution.py:287
  45.0 0.7 %shard_map.51 = f32[3,2,32,128]{3,2,1,0:T(8,128)} custom-call(f32[5,32,128]{2,1,0:T(8,128)S(1)} %get-tuple-element.39.flat, f32[5,32,128]{2,1,0:T(8,128)S(1)} %collective-permute-done.1.flat_rest, f32[2,32,128]{2,1,0:T(8,128)S(1)} %get-tuple-element.45.kept, f32[2,32,128]{2,1,0:T(8,128)S(1)} %collective-permute-done.12.near, ...), custom_call_target="tpu_custom_call" | custom-call | tf_op jit(solution)/shard_map/pallas_call | solution.py:253
  (1 shorter events, 0.0 us)
Async XLA Ops:
  0.0 3.2 %copy-start = (bf16[128,128]{1,0:T(8,128)(2,1)S(1)}, bf16[128,128]{1,0:T(8,128)(2,1)}, u32[]{:S(2)}) copy-start(bf16[128,128]{1,0:T(8,128)(2,1)} %constant.2.clone.rest_9_) | copy-start | bytes 98308
  0.0 3.2 %copy-start.1 = (bf16[128,128]{1,0:T(8,128)(2,1)S(1)}, bf16[128,128]{1,0:T(8,128)(2,1)}, u32[]{:S(2)}) copy-start(bf16[128,128]{1,0:T(8,128)(2,1)} %constant.4.rest_8_) | copy-start | bytes 98308
  0.0 3.2 %copy-start.2 = (f32[16]{0:T(128)S(1)}, f32[16]{0:T(128)}, u32[]{:S(2)}) copy-start(f32[16]{0:T(128)} %weights.1) | copy-start | bytes 196
  7.7 8.9 %collective-permute-start = (f32[2,5,32,128]{3,2,1,0:T(8,128)S(1)}, f32[2,5,32,128]{3,2,1,0:T(8,128)S(1)}, u32[]{:S(2)}, u32[]{:S(2)}) collective-permute-start(f32[2,5,32,128]{3,2,1,0:T(8,128)S(1)} %get-tuple-element.38), channel_id=1, source_target_pairs={{0,8},{1,9},{2,10},{3,11},{4,12},{5,13},{6,14},{7,15},{8,0},{9,1},... | collective-permute-start | bytes 491528 | tf_op jit(solution)/shard_map/ppermute | solution.py:287
  8.2 9.9 %collective-permute-start.11 = (bf16[6,2,2,32,128]{4,3,2,1,0:T(8,128)(2,1)S(1)}, bf16[6,2,2,32,128]{4,3,2,1,0:T(8,128)(2,1)S(1)}, u32[]{:S(2)}, u32[]{:S(2)}) collective-permute-start(bf16[6,2,2,32,128]{4,3,2,1,0:T(8,128)(2,1)S(1)} %get-tuple-element.31.rest_2_.own1), channel_id=1, source_target_pairs={{0,6},{1,3},{2,0},{3,5},{4,2},{5,7},{6,4},{7,1},{8,14},{9,11},{10,... | collective-permute-start | bytes 589832 | tf_op jit(solution)/shard_map/ppermute | solution.py:287
  12.9 2.2 %collective-permute-start.2 = (f32[16,128]{1,0:T(8,128)S(1)}, f32[16,128]{1,0:T(8,128)S(1)}, u32[]{:S(2)}, u32[]{:S(2)}) collective-permute-start(f32[16,128]{1,0:T(8,128)S(1)} %get-tuple-element.41.weights), channel_id=1, source_target_pairs={{0,8},{1,9},{2,10},{3,11},{4,12},{5,13},{6,14},{7,15},{8,0},{9,1},... | collective-permute-start | bytes 24584 | tf_op jit(solution)/shard_map/ppermute | solution.py:287
  13.1 8.1 %collective-permute-start.10 = (bf16[6,2,2,32,128]{4,3,2,1,0:T(8,128)(2,1)S(1)}, bf16[6,2,2,32,128]{4,3,2,1,0:T(8,128)(2,1)S(1)}, u32[]{:S(2)}, u32[]{:S(2)}) collective-permute-start(bf16[6,2,2,32,128]{4,3,2,1,0:T(8,128)(2,1)S(1)} %get-tuple-element.32.rest_3_), channel_id=1, source_target_pairs={{0,1},{1,0},{2,3},{3,2},{4,5},{5,4},{6,7},{7,6},{8,9},{9,8},{10,11... | collective-permute-start | bytes 589832 | tf_op jit(solution)/shard_map/ppermute | solution.py:287
  13.1 14.8 %collective-permute-start.8 = (bf16[10,2,2,32,128]{4,3,2,1,0:T(8,128)(2,1)S(1)}, bf16[10,2,2,32,128]{4,3,2,1,0:T(8,128)(2,1)S(1)}, u32[]{:S(2)}, u32[]{:S(2)}) collective-permute-start(bf16[10,2,2,32,128]{4,3,2,1,0:T(8,128)(2,1)S(1)} %get-tuple-element.29.rest_0_.lead), channel_id=1, source_target_pairs={{0,1},{1,0},{2,3},{3,2},{4,5},{5,7},{6,4},{7,6},{8,9},{9,8},{10,11... | collective-permute-start | bytes 983048 | tf_op jit(solution)/shard_map/ppermute | solution.py:287
  15.1 12.8 %collective-permute-start.9 = (bf16[10,2,2,32,128]{4,3,2,1,0:T(8,128)(2,1)S(1)}, bf16[10,2,2,32,128]{4,3,2,1,0:T(8,128)(2,1)S(1)}, u32[]{:S(2)}, u32[]{:S(2)}) collective-permute-start(bf16[10,2,2,32,128]{4,3,2,1,0:T(8,128)(2,1)S(1)} %get-tuple-element.30.rest_1_.trail), channel_id=1, source_target_pairs={{0,6},{1,3},{2,0},{3,5},{4,2},{5,4},{6,7},{7,1},{8,14},{9,11},{10,... | collective-permute-start | bytes 983048 | tf_op jit(solution)/shard_map/ppermute | solution.py:287
  16.5 11.4 %collective-permute-start.5 = (bf16[10,2,2,32,128]{4,3,2,1,0:T(8,128)(2,1)S(1)}, bf16[10,2,2,32,128]{4,3,2,1,0:T(8,128)(2,1)S(1)}, u32[]{:S(2)}, u32[]{:S(2)}) collective-permute-start(bf16[10,2,2,32,128]{4,3,2,1,0:T(8,128)(2,1)S(1)} %get-tuple-element.33.rest_4_), channel_id=1, source_target_pairs={{0,8},{1,9},{2,10},{3,11},{4,12},{5,13},{6,14},{7,15},{8,0},{9,1},... | collective-permute-start | bytes 983048 | tf_op jit(solution)/shard_map/ppermute | solution.py:287
  18.2 14.0 %collective-permute-start.7 = (bf16[10,2,2,32,128]{4,3,2,1,0:T(8,128)(2,1)S(1)}, bf16[10,2,2,32,128]{4,3,2,1,0:T(8,128)(2,1)S(1)}, u32[]{:S(2)}, u32[]{:S(2)}) collective-permute-start(bf16[10,2,2,32,128]{4,3,2,1,0:T(8,128)(2,1)S(1)} %get-tuple-element.33.rest_4_), channel_id=1, source_target_pairs={{0,14},{1,11},{2,8},{3,13},{4,10},{5,15},{6,12},{7,9},{8,6},{9,3},... | collective-permute-start | bytes 983048 | tf_op jit(solution)/shard_map/ppermute | solution.py:287
  21.1 13.2 %collective-permute-start.6 = (bf16[10,2,2,32,128]{4,3,2,1,0:T(8,128)(2,1)S(1)}, bf16[10,2,2,32,128]{4,3,2,1,0:T(8,128)(2,1)S(1)}, u32[]{:S(2)}, u32[]{:S(2)}) collective-permute-start(bf16[10,2,2,32,128]{4,3,2,1,0:T(8,128)(2,1)S(1)} %get-tuple-element.34.rest_5_), channel_id=1, source_target_pairs={{0,9},{1,8},{2,11},{3,10},{4,13},{5,12},{6,15},{7,14},{8,1},{9,0},... | collective-permute-start | bytes 983048 | tf_op jit(solution)/shard_map/ppermute | solution.py:287
  27.8 6.8 %collective-permute-start.3 = (bf16[6,2,2,32,128]{4,3,2,1,0:T(8,128)(2,1)S(1)}, bf16[6,2,2,32,128]{4,3,2,1,0:T(8,128)(2,1)S(1)}, u32[]{:S(2)}, u32[]{:S(2)}) collective-permute-start(bf16[6,2,2,32,128]{4,3,2,1,0:T(8,128)(2,1)S(1)} %get-tuple-element.35.rest_6_), channel_id=1, source_target_pairs={{0,8},{1,9},{2,10},{3,11},{4,12},{5,13},{6,14},{7,15},{8,0},{9,1},... | collective-permute-start | bytes 589832 | tf_op jit(solution)/shard_map/ppermute | solution.py:287
  27.9 10.0 %collective-permute-start.4 = (bf16[6,2,2,32,128]{4,3,2,1,0:T(8,128)(2,1)S(1)}, bf16[6,2,2,32,128]{4,3,2,1,0:T(8,128)(2,1)S(1)}, u32[]{:S(2)}, u32[]{:S(2)}) collective-permute-start(bf16[6,2,2,32,128]{4,3,2,1,0:T(8,128)(2,1)S(1)} %get-tuple-element.36.rest_7_), channel_id=1, source_target_pairs={{0,9},{1,8},{2,11},{3,10},{4,13},{5,12},{6,15},{7,14},{8,1},{9,0},... | collective-permute-start | bytes 589832 | tf_op jit(solution)/shard_map/ppermute | solution.py:287
  28.0 10.0 %collective-permute-start.13 = (bf16[6,2,2,32,128]{4,3,2,1,0:T(8,128)(2,1)S(1)}, bf16[6,2,2,32,128]{4,3,2,1,0:T(8,128)(2,1)S(1)}, u32[]{:S(2)}, u32[]{:S(2)}) collective-permute-start(bf16[6,2,2,32,128]{4,3,2,1,0:T(8,128)(2,1)S(1)} %get-tuple-element.35.rest_6_), channel_id=1, source_target_pairs={{0,14},{1,11},{2,8},{3,13},{4,10},{5,15},{6,12},{7,9},{8,6},{9,3},... | collective-permute-start | bytes 589832 | tf_op jit(solution)/shard_map/ppermute | solution.py:287
  32.2 8.8 %collective-permute-start.1 = (f32[5,32,128]{2,1,0:T(8,128)S(1)}, f32[5,32,128]{2,1,0:T(8,128)S(1)}, u32[]{:S(2)}, u32[]{:S(2)}) collective-permute-start(f32[5,32,128]{2,1,0:T(8,128)S(1)} %get-tuple-element.40), channel_id=1, source_target_pairs={{0,16},{1,17},{2,18},{3,19},{4,20},{5,21},{6,22},{7,23},{8,24},{9,... | collective-permute-start | bytes 245768 | tf_op jit(solution)/shard_map/ppermute | solution.py:287
  38.1 4.9 %collective-permute-start.14 = (f32[2,32,128]{2,1,0:T(8,128)S(1)}, f32[2,32,128]{2,1,0:T(8,128)S(1)}, u32[]{:S(2)}, u32[]{:S(2)}) collective-permute-start(f32[2,32,128]{2,1,0:T(8,128)S(1)} %get-tuple-element.49), channel_id=1, source_target_pairs={{0,18},{1,7},{2,20},{3,2},{4,22},{5,4},{6,16},{7,5},{8,26},{9,15},... | collective-permute-start | bytes 98312 | tf_op jit(solution)/shard_map/ppermute | solution.py:287
  38.6 4.3 %collective-permute-start.15 = (f32[2,32,128]{2,1,0:T(8,128)S(1)}, f32[2,32,128]{2,1,0:T(8,128)S(1)}, u32[]{:S(2)}, u32[]{:S(2)}) collective-permute-start(f32[2,32,128]{2,1,0:T(8,128)S(1)} %get-tuple-element.50), channel_id=1, source_target_pairs={{0,17},{1,0},{2,19},{3,1},{4,21},{5,3},{6,23},{7,6},{8,25},{9,8},{... | collective-permute-start | bytes 98312 | tf_op jit(solution)/shard_map/ppermute | solution.py:287
  41.1 3.9 %collective-permute-start.12 = (f32[2,32,128]{2,1,0:T(8,128)S(1)}, f32[2,32,128]{2,1,0:T(8,128)S(1)}, u32[]{:S(2)}, u32[]{:S(2)}) collective-permute-start(f32[2,32,128]{2,1,0:T(8,128)S(1)} %get-tuple-element.46), channel_id=1, source_target_pairs={{0,16},{1,0},{2,18},{3,2},{4,20},{5,4},{6,22},{7,6},{8,24},{9,8},{... | collective-permute-start | bytes 98312 | tf_op jit(solution)/shard_map/ppermute | solution.py:287

commit v3 on v2

--- a/solution.py
+++ b/solution.py
@@ -9,7 +9,7 @@
 from jax.sharding import PartitionSpec as P
 
 
-ODD, CORNER, CORE, HALF, SWAP, OWN, SIDE = range(4, 11)
+ODD, CORNER, CORE, HALF, SWAP, OWN, SIDE, RIDE = range(4, 12)
 
 
 def stencil(cells):
@@ -118,7 +118,9 @@
     for slab in CELLS:
         at = lax.axis_index("grid") == slab % lax.axis_size("grid")
         ahead = jnp.where(at, 1 - ahead, ahead)
-    return quarters + (odd, corner, core, half, ahead, own, side)
+    level = lax.axis_index("grid") // 2
+    ride = jnp.where((level > 0) & (level < lax.axis_size("grid") // 2 - 1), corner, 0)
+    return quarters + (odd, corner, core, half, ahead, own, side, ride)
 
 
 def split_kernel(pieces, orbitals, *rest):
@@ -229,10 +231,12 @@
     shape = kept.shape[1:]
     odd = flag(flags, ODD, shape)
     here = flag(flags, CORNER, shape)
+    ride = flag(flags, RIDE, shape)
     own_parts, side_parts = scaled(odd, edges(weights, offset, own, side, sums))
     for plane in range(2):
         kept[plane] = jnp.where(here, own_parts[plane], 0.0)
-        near[plane] = jnp.where(here, side_parts[plane], own_parts[plane])
+        part = jnp.where(here, side_parts[plane], own_parts[plane])
+        near[plane] = jnp.where(ride, 0.0, part)
         inner_side[plane] = side_parts[plane]
 
 
@@ -240,10 +244,11 @@
     shape = middle.shape[1:]
     odd = flag(flags, ODD, shape)
     here = flag(flags, CORNER, shape)
+    ride = flag(flags, RIDE, shape)
     side_parts, far_parts = scaled(odd, edges(weights, offset, side, far, sums))
     ahead = flag(flags, SWAP, shape)
     for plane in range(2):
-        beside = side_parts[plane] + jnp.where(here, 0.0, inner_side[plane])
+        beside = side_parts[plane] + jnp.where(here & ~ride, 0.0, inner_side[plane])
         middle[plane] = jnp.where(ahead, beside, far_parts[plane])
         distant[plane] = jnp.where(ahead, far_parts[plane], beside)
 
@@ -332,7 +337,11 @@
     def is_corner(b, g):
         return b // 2 != g % 2
 
-    got_near = route(near, lambda b, g: (b, g ^ 1) if is_corner(b, g) else (b ^ 2, g))
+    def near_goal(b, g):
+        inside_z = 0 < g // 2 < slabs // 2 - 1
+        return (b, g ^ 1) if is_corner(b, g) and not inside_z else (b ^ 2, g)
+
+    got_near = route(near, near_goal)
     middle, distant = call(
         functools.partial(outer_kernel, cut),
         (flags, w2, side[3], far[3], outer, inner_side),
@@ -356,10 +365,10 @@
 
 
 FIRST = (-1,)
-CELLS = (1, -1)
+CELLS = (1, 5, -1)
 UNROLL = 4
 FIRST = (-1,)
-CELLS = (1, -1)
+CELLS = (1, 5, -1)
 
 
 def solution(mesh):

time: 45.8 us -> 45.8 us (level)
  no operation moved by 1% of the time
where the time goes in v3:
time: 45.8 us; the launch traced here: 45.6 us
  waiting for transfers between devices  18.3 us (40%)
  starting transfers between devices  17.8 us (39%)
  Pallas kernels  9.43 us (21%)
    ppermute x16, waiting for transfers between devices, route(): return lax.ppermute(value, ('band', 'grid'), pairs)  18.3 us
    ppermute x16, starting transfers between devices, route(): return lax.ppermute(value, ('band', 'grid'), pairs)  17.8 us
    pallas_call x1, Pallas kernels, lateral(): pl.pallas_call(functools.partial(lateral_kernel, pieces), in_specs=[smem]...  4.42 us
    pallas_call x2, Pallas kernels, split(): pl.pallas_call(functools.partial(split_kernel, pieces), in_specs=[pl.Bloc...  3.17 us
    pallas_call x6, Pallas kernels, call(): pl.pallas_call(kernel, in_specs=[vmem] * len(arrays), out_specs=[vmem] *...  1.84 us
  transfers between devices with their start and end apart: 16, of which 6 were waited for; matrix products, arithmetic and copies ran while one was open for 0% of the time, Pallas kernels for 3%

profile of v3, /device:TPU:0, one launch (start us, length us, event | category | flops | bytes accessed | tf_op | source)
XLA Modules:
  0.0 45.6 jit_solution(3866898558714039516)
XLA Ops:
  0.0 0.0 copy-start
  0.0 0.0 copy-start.1
  0.0 0.0 copy-start.2
  0.0 2.1 %split.3 = (bf16[6,2,2,32,128]{4,3,2,1,0:T(8,128)(2,1)S(1)}, bf16[6,2,2,32,128]{4,3,2,1,0:T(8,128)(2,1)S(1)}, bf16[10,2,2,32,128]{4,3,2,1,0:T(8,128)(2,1)S(1)}, ...) custom-call(bf16[16,2,2,128,128]{4,3,2,1,0:T(8,128)(2,1)} %orbitals.3), custom_call_target="tpu_custom_call" | custom-call | tf_op jit(solution)/shard_map/split/pallas_call | solution.py:151
  2.1 1.1 %split.2 = (bf16[10,2,2,32,128]{4,3,2,1,0:T(8,128)(2,1)S(1)}, bf16[10,2,2,32,128]{4,3,2,1,0:T(8,128)(2,1)S(1)}, s32[16,128]{1,0:T(8,128)S(1)}) custom-call(bf16[16,2,2,128,128]{4,3,2,1,0:T(8,128)(2,1)} %orbitals.3), custom_call_target="tpu_custom_call" | custom-call | tf_op jit(solution)/shard_map/split/pallas_call | solution.py:151
  3.2 0.0 copy-done
  3.2 0.0 copy-done.1
  3.2 0.0 copy-done.2
  3.2 4.4 %lateral.1 = (f32[2,5,32,128]{3,2,1,0:T(8,128)S(1)}, f32[2,5,32,128]{3,2,1,0:T(8,128)S(1)}, f32[16,128]{1,0:T(8,128)S(1)}) custom-call(f32[16]{0:T(128)S(1)} %copy-done.2, bf16[10,2,2,32,128]{4,3,2,1,0:T(8,128)(2,1)S(1)} %get-tuple-element.29.rest_0_.lead, bf16[10,2,2,32,128]{4,3,2,1,0:T(8,128)(2,1)S(1)} %get-tuple-element.30.rest_1_.trail, ...), custom_call_target="tpu_custom_call" | custom-call | tf_op jit(solution)/shard_map/lateral/pallas_call | solution.py:69
  7.7 0.6 %collective-permute-start = (f32[2,5,32,128]{3,2,1,0:T(8,128)S(1)}, f32[2,5,32,128]{3,2,1,0:T(8,128)S(1)}, u32[]{:S(2)}, u32[]{:S(2)}) collective-permute-start(f32[2,5,32,128]{3,2,1,0:T(8,128)S(1)} %get-tuple-element.38), channel_id=1, source_target_pairs={{0,8},{1,9},{2,10},{3,11},{4,12},{5,13},{6,14},{7,15},{8,0},{9,1},... | collective-permute-start | bytes 491528 | tf_op jit(solution)/shard_map/ppermute | solution.py:292
  8.2 4.7 %collective-permute-start.11 = (bf16[6,2,2,32,128]{4,3,2,1,0:T(8,128)(2,1)S(1)}, bf16[6,2,2,32,128]{4,3,2,1,0:T(8,128)(2,1)S(1)}, u32[]{:S(2)}, u32[]{:S(2)}) collective-permute-start(bf16[6,2,2,32,128]{4,3,2,1,0:T(8,128)(2,1)S(1)} %get-tuple-element.31.rest_2_.own1), channel_id=1, source_target_pairs={{0,6},{1,3},{2,0},{3,5},{4,2},{5,7},{6,4},{7,1},{8,14},{9,11},{10,... | collective-permute-start | bytes 589832 | tf_op jit(solution)/shard_map/ppermute | solution.py:292
  12.9 0.2 collective-permute-start.2
  13.1 0.0 collective-permute-start.10
  13.1 2.0 %collective-permute-start.8 = (bf16[10,2,2,32,128]{4,3,2,1,0:T(8,128)(2,1)S(1)}, bf16[10,2,2,32,128]{4,3,2,1,0:T(8,128)(2,1)S(1)}, u32[]{:S(2)}, u32[]{:S(2)}) collective-permute-start(bf16[10,2,2,32,128]{4,3,2,1,0:T(8,128)(2,1)S(1)} %get-tuple-element.29.rest_0_.lead), channel_id=1, source_target_pairs={{0,1},{1,0},{2,3},{3,2},{4,5},{5,7},{6,4},{7,6},{8,9},{9,8},{10,11... | collective-permute-start | bytes 983048 | tf_op jit(solution)/shard_map/ppermute | solution.py:292
  15.1 0.0 collective-permute-done.2.weights
  15.1 1.5 %collective-permute-start.9 = (bf16[10,2,2,32,128]{4,3,2,1,0:T(8,128)(2,1)S(1)}, bf16[10,2,2,32,128]{4,3,2,1,0:T(8,128)(2,1)S(1)}, u32[]{:S(2)}, u32[]{:S(2)}) collective-permute-start(bf16[10,2,2,32,128]{4,3,2,1,0:T(8,128)(2,1)S(1)} %get-tuple-element.30.rest_1_.trail), channel_id=1, source_target_pairs={{0,6},{1,3},{2,0},{3,5},{4,2},{5,4},{6,7},{7,1},{8,14},{9,11},{10,... | collective-permute-start | bytes 983048 | tf_op jit(solution)/shard_map/ppermute | solution.py:292
  16.5 0.0 collective-permute-done.theirs
  16.5 0.0 collective-permute-start.5
  16.5 1.6 %collective-permute-done.11.far1 = bf16[6,2,2,32,128]{4,3,2,1,0:T(8,128)(2,1)S(1)} collective-permute-done((bf16[6,2,2,32,128]{4,3,2,1,0:T(8,128)(2,1)S(1)}, bf16[6,2,2,32,128]{4,3,2,1,0:T(8,128)(2,1)S(1)}, u32[]{:S(2)}, u32[]{:S(2)}) %collective-permute-start.11) | collective-permute-done | bytes 196640 | tf_op jit(solution)/shard_map/ppermute | solution.py:292
  18.2 3.0 %collective-permute-start.7 = (bf16[10,2,2,32,128]{4,3,2,1,0:T(8,128)(2,1)S(1)}, bf16[10,2,2,32,128]{4,3,2,1,0:T(8,128)(2,1)S(1)}, u32[]{:S(2)}, u32[]{:S(2)}) collective-permute-start(bf16[10,2,2,32,128]{4,3,2,1,0:T(8,128)(2,1)S(1)} %get-tuple-element.33.rest_4_), channel_id=1, source_target_pairs={{0,14},{1,11},{2,8},{3,13},{4,10},{5,15},{6,12},{7,9},{8,6},{9,3},... | collective-permute-start | bytes 983048 | tf_op jit(solution)/shard_map/ppermute | solution.py:292
  21.1 0.0 collective-permute-done.10.side1
  21.1 0.0 collective-permute-start.6
  21.1 6.7 %collective-permute-done.8.got_lead = bf16[10,2,2,32,128]{4,3,2,1,0:T(8,128)(2,1)S(1)} collective-permute-done((bf16[10,2,2,32,128]{4,3,2,1,0:T(8,128)(2,1)S(1)}, bf16[10,2,2,32,128]{4,3,2,1,0:T(8,128)(2,1)S(1)}, u32[]{:S(2)}, u32[]{:S(2)}) %collective-permute-start.8) | collective-permute-done | bytes 327712 | tf_op jit(solution)/shard_map/ppermute | solution.py:292
  27.8 0.0 collective-permute-start.3
  27.9 0.0 collective-permute-done.9.got_trail
  27.9 0.1 collective-permute-start.4
  28.0 0.0 collective-permute-done.5.own
  28.0 1.3 %collective-permute-start.13 = (bf16[6,2,2,32,128]{4,3,2,1,0:T(8,128)(2,1)S(1)}, bf16[6,2,2,32,128]{4,3,2,1,0:T(8,128)(2,1)S(1)}, u32[]{:S(2)}, u32[]{:S(2)}) collective-permute-start(bf16[6,2,2,32,128]{4,3,2,1,0:T(8,128)(2,1)S(1)} %get-tuple-element.35.rest_6_), channel_id=1, source_target_pairs={{0,14},{1,11},{2,8},{3,13},{4,10},{5,15},{6,12},{7,9},{8,6},{9,3},... | collective-permute-start | bytes 589832 | tf_op jit(solution)/shard_map/ppermute | solution.py:292
  29.3 2.9 %collective-permute-done.7.far = bf16[10,2,2,32,128]{4,3,2,1,0:T(8,128)(2,1)S(1)} collective-permute-done((bf16[10,2,2,32,128]{4,3,2,1,0:T(8,128)(2,1)S(1)}, bf16[10,2,2,32,128]{4,3,2,1,0:T(8,128)(2,1)S(1)}, u32[]{:S(2)}, u32[]{:S(2)}) %collective-permute-start.7) | collective-permute-done | bytes 327712 | tf_op jit(solution)/shard_map/ppermute | solution.py:292
  32.2 1.5 %collective-permute-start.1 = (f32[5,32,128]{2,1,0:T(8,128)S(1)}, f32[5,32,128]{2,1,0:T(8,128)S(1)}, u32[]{:S(2)}, u32[]{:S(2)}) collective-permute-start(f32[5,32,128]{2,1,0:T(8,128)S(1)} %get-tuple-element.40), channel_id=1, source_target_pairs={{0,16},{1,17},{2,18},{3,19},{4,20},{5,21},{6,22},{7,23},{8,24},{9,... | collective-permute-start | bytes 245768 | tf_op jit(solution)/shard_map/ppermute | solution.py:292
  33.7 0.6 %shard_map.47 = (f32[4,32,128]{2,1,0:T(8,128)S(1)}, f32[4,32,128]{2,1,0:T(8,128)S(1)}) custom-call(f32[16,128]{1,0:T(8,128)S(1)} %get-tuple-element.41.weights, bf16[10,2,2,32,128]{4,3,2,1,0:T(8,128)(2,1)S(1)} %get-tuple-element.29.rest_0_.lead, bf16[10,2,2,32,128]{4,3,2,1,0:T(8,128)(2,1)S(1)} %get-tuple-element.30.rest_1_.trail, ...), custom_call_target="tpu_custom_call" | custom-call | tf_op jit(solution)/shard_map/pallas_call | solution.py:258
  34.3 0.0 collective-permute-done.6.side
  34.3 0.4 shard_map.48
  34.7 0.0 collective-permute-done.3.own
  34.7 3.2 %collective-permute-done.4.side = bf16[6,2,2,32,128]{4,3,2,1,0:T(8,128)(2,1)S(1)} collective-permute-done((bf16[6,2,2,32,128]{4,3,2,1,0:T(8,128)(2,1)S(1)}, bf16[6,2,2,32,128]{4,3,2,1,0:T(8,128)(2,1)S(1)}, u32[]{:S(2)}, u32[]{:S(2)}) %collective-permute-start.4) | collective-permute-done | bytes 196640 | tf_op jit(solution)/shard_map/ppermute | solution.py:292
  37.8 0.1 shard_map.49
  38.0 0.0 collective-permute-done.13.far
  38.0 0.1 shard_map.50
  38.1 0.6 %collective-permute-start.14 = (f32[2,32,128]{2,1,0:T(8,128)S(1)}, f32[2,32,128]{2,1,0:T(8,128)S(1)}, u32[]{:S(2)}, u32[]{:S(2)}) collective-permute-start(f32[2,32,128]{2,1,0:T(8,128)S(1)} %get-tuple-element.49), channel_id=1, source_target_pairs={{0,18},{1,7},{2,20},{3,2},{4,22},{5,3},{6,16},{7,5},{8,26},{9,15},... | collective-permute-start | bytes 98312 | tf_op jit(solution)/shard_map/ppermute | solution.py:292
  38.6 2.4 %collective-permute-start.15 = (f32[2,32,128]{2,1,0:T(8,128)S(1)}, f32[2,32,128]{2,1,0:T(8,128)S(1)}, u32[]{:S(2)}, u32[]{:S(2)}) collective-permute-start(f32[2,32,128]{2,1,0:T(8,128)S(1)} %get-tuple-element.50), channel_id=1, source_target_pairs={{0,17},{1,0},{2,19},{3,1},{4,21},{5,4},{6,23},{7,6},{8,25},{9,8},{... | collective-permute-start | bytes 98312 | tf_op jit(solution)/shard_map/ppermute | solution.py:292
  41.1 0.0 collective-permute-start.12
  41.1 0.0 collective-permute-done.1.flat_rest
  41.1 1.9 %collective-permute-done.14.middle = f32[2,32,128]{2,1,0:T(8,128)S(1)} collective-permute-done((f32[2,32,128]{2,1,0:T(8,128)S(1)}, f32[2,32,128]{2,1,0:T(8,128)S(1)}, u32[]{:S(2)}, u32[]{:S(2)}) %collective-permute-start.14) | collective-permute-done | bytes 32800 | tf_op jit(solution)/shard_map/ppermute | solution.py:292
  43.0 0.0 collective-permute-done.15.distant
  43.0 2.0 %collective-permute-done.12.near = f32[2,32,128]{2,1,0:T(8,128)S(1)} collective-permute-done((f32[2,32,128]{2,1,0:T(8,128)S(1)}, f32[2,32,128]{2,1,0:T(8,128)S(1)}, u32[]{:S(2)}, u32[]{:S(2)}) %collective-permute-start.12) | collective-permute-done | bytes 32800 | tf_op jit(solution)/shard_map/ppermute | solution.py:292
  45.0 0.7 %shard_map.51 = f32[3,2,32,128]{3,2,1,0:T(8,128)} custom-call(f32[5,32,128]{2,1,0:T(8,128)S(1)} %get-tuple-element.39.flat, f32[5,32,128]{2,1,0:T(8,128)S(1)} %collective-permute-done.1.flat_rest, f32[2,32,128]{2,1,0:T(8,128)S(1)} %get-tuple-element.45.kept, f32[2,32,128]{2,1,0:T(8,128)S(1)} %collective-permute-done.12.near, ...), custom_call_target="tpu_custom_call" | custom-call | tf_op jit(solution)/shard_map/pallas_call | solution.py:258
  (1 shorter events, 0.0 us)
Async XLA Ops:
  0.0 3.2 %copy-start = (bf16[128,128]{1,0:T(8,128)(2,1)S(1)}, bf16[128,128]{1,0:T(8,128)(2,1)}, u32[]{:S(2)}) copy-start(bf16[128,128]{1,0:T(8,128)(2,1)} %constant.2.clone.rest_9_) | copy-start | bytes 98308
  0.0 3.2 %copy-start.1 = (bf16[128,128]{1,0:T(8,128)(2,1)S(1)}, bf16[128,128]{1,0:T(8,128)(2,1)}, u32[]{:S(2)}) copy-start(bf16[128,128]{1,0:T(8,128)(2,1)} %constant.4.rest_8_) | copy-start | bytes 98308
  0.0 3.2 %copy-start.2 = (f32[16]{0:T(128)S(1)}, f32[16]{0:T(128)}, u32[]{:S(2)}) copy-start(f32[16]{0:T(128)} %weights.1) | copy-start | bytes 196
  7.7 8.9 %collective-permute-start = (f32[2,5,32,128]{3,2,1,0:T(8,128)S(1)}, f32[2,5,32,128]{3,2,1,0:T(8,128)S(1)}, u32[]{:S(2)}, u32[]{:S(2)}) collective-permute-start(f32[2,5,32,128]{3,2,1,0:T(8,128)S(1)} %get-tuple-element.38), channel_id=1, source_target_pairs={{0,8},{1,9},{2,10},{3,11},{4,12},{5,13},{6,14},{7,15},{8,0},{9,1},... | collective-permute-start | bytes 491528 | tf_op jit(solution)/shard_map/ppermute | solution.py:292
  8.2 9.9 %collective-permute-start.11 = (bf16[6,2,2,32,128]{4,3,2,1,0:T(8,128)(2,1)S(1)}, bf16[6,2,2,32,128]{4,3,2,1,0:T(8,128)(2,1)S(1)}, u32[]{:S(2)}, u32[]{:S(2)}) collective-permute-start(bf16[6,2,2,32,128]{4,3,2,1,0:T(8,128)(2,1)S(1)} %get-tuple-element.31.rest_2_.own1), channel_id=1, source_target_pairs={{0,6},{1,3},{2,0},{3,5},{4,2},{5,7},{6,4},{7,1},{8,14},{9,11},{10,... | collective-permute-start | bytes 589832 | tf_op jit(solution)/shard_map/ppermute | solution.py:292
  12.9 2.2 %collective-permute-start.2 = (f32[16,128]{1,0:T(8,128)S(1)}, f32[16,128]{1,0:T(8,128)S(1)}, u32[]{:S(2)}, u32[]{:S(2)}) collective-permute-start(f32[16,128]{1,0:T(8,128)S(1)} %get-tuple-element.41.weights), channel_id=1, source_target_pairs={{0,8},{1,9},{2,10},{3,11},{4,12},{5,13},{6,14},{7,15},{8,0},{9,1},... | collective-permute-start | bytes 24584 | tf_op jit(solution)/shard_map/ppermute | solution.py:292
  13.1 8.1 %collective-permute-start.10 = (bf16[6,2,2,32,128]{4,3,2,1,0:T(8,128)(2,1)S(1)}, bf16[6,2,2,32,128]{4,3,2,1,0:T(8,128)(2,1)S(1)}, u32[]{:S(2)}, u32[]{:S(2)}) collective-permute-start(bf16[6,2,2,32,128]{4,3,2,1,0:T(8,128)(2,1)S(1)} %get-tuple-element.32.rest_3_), channel_id=1, source_target_pairs={{0,1},{1,0},{2,3},{3,2},{4,5},{5,4},{6,7},{7,6},{8,9},{9,8},{10,11... | collective-permute-start | bytes 589832 | tf_op jit(solution)/shard_map/ppermute | solution.py:292
  13.1 14.8 %collective-permute-start.8 = (bf16[10,2,2,32,128]{4,3,2,1,0:T(8,128)(2,1)S(1)}, bf16[10,2,2,32,128]{4,3,2,1,0:T(8,128)(2,1)S(1)}, u32[]{:S(2)}, u32[]{:S(2)}) collective-permute-start(bf16[10,2,2,32,128]{4,3,2,1,0:T(8,128)(2,1)S(1)} %get-tuple-element.29.rest_0_.lead), channel_id=1, source_target_pairs={{0,1},{1,0},{2,3},{3,2},{4,5},{5,7},{6,4},{7,6},{8,9},{9,8},{10,11... | collective-permute-start | bytes 983048 | tf_op jit(solution)/shard_map/ppermute | solution.py:292
  15.1 12.8 %collective-permute-start.9 = (bf16[10,2,2,32,128]{4,3,2,1,0:T(8,128)(2,1)S(1)}, bf16[10,2,2,32,128]{4,3,2,1,0:T(8,128)(2,1)S(1)}, u32[]{:S(2)}, u32[]{:S(2)}) collective-permute-start(bf16[10,2,2,32,128]{4,3,2,1,0:T(8,128)(2,1)S(1)} %get-tuple-element.30.rest_1_.trail), channel_id=1, source_target_pairs={{0,6},{1,3},{2,0},{3,5},{4,2},{5,4},{6,7},{7,1},{8,14},{9,11},{10,... | collective-permute-start | bytes 983048 | tf_op jit(solution)/shard_map/ppermute | solution.py:292
  16.5 11.4 %collective-permute-start.5 = (bf16[10,2,2,32,128]{4,3,2,1,0:T(8,128)(2,1)S(1)}, bf16[10,2,2,32,128]{4,3,2,1,0:T(8,128)(2,1)S(1)}, u32[]{:S(2)}, u32[]{:S(2)}) collective-permute-start(bf16[10,2,2,32,128]{4,3,2,1,0:T(8,128)(2,1)S(1)} %get-tuple-element.33.rest_4_), channel_id=1, source_target_pairs={{0,8},{1,9},{2,10},{3,11},{4,12},{5,13},{6,14},{7,15},{8,0},{9,1},... | collective-permute-start | bytes 983048 | tf_op jit(solution)/shard_map/ppermute | solution.py:292
  18.2 14.0 %collective-permute-start.7 = (bf16[10,2,2,32,128]{4,3,2,1,0:T(8,128)(2,1)S(1)}, bf16[10,2,2,32,128]{4,3,2,1,0:T(8,128)(2,1)S(1)}, u32[]{:S(2)}, u32[]{:S(2)}) collective-permute-start(bf16[10,2,2,32,128]{4,3,2,1,0:T(8,128)(2,1)S(1)} %get-tuple-element.33.rest_4_), channel_id=1, source_target_pairs={{0,14},{1,11},{2,8},{3,13},{4,10},{5,15},{6,12},{7,9},{8,6},{9,3},... | collective-permute-start | bytes 983048 | tf_op jit(solution)/shard_map/ppermute | solution.py:292
  21.1 13.2 %collective-permute-start.6 = (bf16[10,2,2,32,128]{4,3,2,1,0:T(8,128)(2,1)S(1)}, bf16[10,2,2,32,128]{4,3,2,1,0:T(8,128)(2,1)S(1)}, u32[]{:S(2)}, u32[]{:S(2)}) collective-permute-start(bf16[10,2,2,32,128]{4,3,2,1,0:T(8,128)(2,1)S(1)} %get-tuple-element.34.rest_5_), channel_id=1, source_target_pairs={{0,9},{1,8},{2,11},{3,10},{4,13},{5,12},{6,15},{7,14},{8,1},{9,0},... | collective-permute-start | bytes 983048 | tf_op jit(solution)/shard_map/ppermute | solution.py:292
  27.8 6.8 %collective-permute-start.3 = (bf16[6,2,2,32,128]{4,3,2,1,0:T(8,128)(2,1)S(1)}, bf16[6,2,2,32,128]{4,3,2,1,0:T(8,128)(2,1)S(1)}, u32[]{:S(2)}, u32[]{:S(2)}) collective-permute-start(bf16[6,2,2,32,128]{4,3,2,1,0:T(8,128)(2,1)S(1)} %get-tuple-element.35.rest_6_), channel_id=1, source_target_pairs={{0,8},{1,9},{2,10},{3,11},{4,12},{5,13},{6,14},{7,15},{8,0},{9,1},... | collective-permute-start | bytes 589832 | tf_op jit(solution)/shard_map/ppermute | solution.py:292
  27.9 10.0 %collective-permute-start.4 = (bf16[6,2,2,32,128]{4,3,2,1,0:T(8,128)(2,1)S(1)}, bf16[6,2,2,32,128]{4,3,2,1,0:T(8,128)(2,1)S(1)}, u32[]{:S(2)}, u32[]{:S(2)}) collective-permute-start(bf16[6,2,2,32,128]{4,3,2,1,0:T(8,128)(2,1)S(1)} %get-tuple-element.36.rest_7_), channel_id=1, source_target_pairs={{0,9},{1,8},{2,11},{3,10},{4,13},{5,12},{6,15},{7,14},{8,1},{9,0},... | collective-permute-start | bytes 589832 | tf_op jit(solution)/shard_map/ppermute | solution.py:292
  28.0 10.0 %collective-permute-start.13 = (bf16[6,2,2,32,128]{4,3,2,1,0:T(8,128)(2,1)S(1)}, bf16[6,2,2,32,128]{4,3,2,1,0:T(8,128)(2,1)S(1)}, u32[]{:S(2)}, u32[]{:S(2)}) collective-permute-start(bf16[6,2,2,32,128]{4,3,2,1,0:T(8,128)(2,1)S(1)} %get-tuple-element.35.rest_6_), channel_id=1, source_target_pairs={{0,14},{1,11},{2,8},{3,13},{4,10},{5,15},{6,12},{7,9},{8,6},{9,3},... | collective-permute-start | bytes 589832 | tf_op jit(solution)/shard_map/ppermute | solution.py:292
  32.2 8.9 %collective-permute-start.1 = (f32[5,32,128]{2,1,0:T(8,128)S(1)}, f32[5,32,128]{2,1,0:T(8,128)S(1)}, u32[]{:S(2)}, u32[]{:S(2)}) collective-permute-start(f32[5,32,128]{2,1,0:T(8,128)S(1)} %get-tuple-element.40), channel_id=1, source_target_pairs={{0,16},{1,17},{2,18},{3,19},{4,20},{5,21},{6,22},{7,23},{8,24},{9,... | collective-permute-start | bytes 245768 | tf_op jit(solution)/shard_map/ppermute | solution.py:292
  38.1 4.9 %collective-permute-start.14 = (f32[2,32,128]{2,1,0:T(8,128)S(1)}, f32[2,32,128]{2,1,0:T(8,128)S(1)}, u32[]{:S(2)}, u32[]{:S(2)}) collective-permute-start(f32[2,32,128]{2,1,0:T(8,128)S(1)} %get-tuple-element.49), channel_id=1, source_target_pairs={{0,18},{1,7},{2,20},{3,2},{4,22},{5,3},{6,16},{7,5},{8,26},{9,15},... | collective-permute-start | bytes 98312 | tf_op jit(solution)/shard_map/ppermute | solution.py:292
  38.6 4.3 %collective-permute-start.15 = (f32[2,32,128]{2,1,0:T(8,128)S(1)}, f32[2,32,128]{2,1,0:T(8,128)S(1)}, u32[]{:S(2)}, u32[]{:S(2)}) collective-permute-start(f32[2,32,128]{2,1,0:T(8,128)S(1)} %get-tuple-element.50), channel_id=1, source_target_pairs={{0,17},{1,0},{2,19},{3,1},{4,21},{5,4},{6,23},{7,6},{8,25},{9,8},{... | collective-permute-start | bytes 98312 | tf_op jit(solution)/shard_map/ppermute | solution.py:292
  41.1 3.9 %collective-permute-start.12 = (f32[2,32,128]{2,1,0:T(8,128)S(1)}, f32[2,32,128]{2,1,0:T(8,128)S(1)}, u32[]{:S(2)}, u32[]{:S(2)}) collective-permute-start(f32[2,32,128]{2,1,0:T(8,128)S(1)} %get-tuple-element.46), channel_id=1, source_target_pairs={{0,16},{1,0},{2,18},{3,19},{4,20},{5,21},{6,22},{7,6},{8,24},{9,8}... | collective-permute-start | bytes 98312 | tf_op jit(solution)/shard_map/ppermute | solution.py:292
